TPU v7x, 256 devices: a whole 4x4x8 slice. The times are simulated.
256 devices in a mesh: section: 8 (over y, x_lo), dev: 32 (over x_hi, z, core).
Axes of the slice: x: 4 (x_hi: 2, x_lo: 2; x = x_hi * 2 + x_lo), y: 4, z: 8, core: 2. Of those that a mesh axis runs over, the one named last changes fastest.
Arguments:
- late_sent: bfloat16 [8, 3136, 1024], P('section', 'dev'), may hold values from -5 to 5
- entry_rows: bfloat16 [3136, 1024], P('dev'), may hold values from -5 to 5
- gain_first: float32 [8, 1024], P('section'), may hold values from 0.1 to 1.9
- shift_first: float32 [8, 1024], P('section'), may hold values from -3 to 3
- expand_late: bfloat16 [8, 1024, 4096], P('section', None, 'dev'), may hold values from -0.1875 to 0.1875
- gain_inner: float32 [8, 4096], P('section', 'dev'), may hold values from 0.1 to 1.9
- shift_inner: float32 [8, 4096], P('section', 'dev'), may hold values from -3 to 3
- reduce_late: bfloat16 [8, 4096, 1024], P('section', 'dev'), may hold values from -0.09375 to 0.09375
- early_saved: bfloat16 [8, 50176, 256], P('section', 'dev'), may hold values from -6 to 6
- upstream_grad: bfloat16 [8, 50176, 256], P('section', 'dev'), may hold values from -6 to 6
- exit_grad: bfloat16 [50176, 256], P('dev'), may hold values from -6 to 6
- expand_early: bfloat16 [8, 256, 1024], P('section'), may hold values from -0.375 to 0.375
- reduce_early: bfloat16 [8, 1024, 256], P('section'), may hold values from -0.1875 to 0.1875
Outputs:
- late_out: bfloat16 [8, 3136, 1024], P('section', 'dev')
- input_grad: bfloat16 [8, 50176, 256], P('section', 'dev')
- grad_expand: float32 [8, 256, 1024], P('section')
- grad_reduce: float32 [8, 1024, 256], P('section')
All inputs are finite; a program needn't handle non-finite values.
Results may differ from a plain program's by a relative error of at most 0.02.
Values may be sent and summed in bfloat16 or wider, within the bound.
A program may use at most 128 MiB of HBM per device.

v0:
```python
import math

import jax
import jax.numpy as jnp
from jax import lax
from jax.sharding import Mesh
from jax.sharding import PartitionSpec as P

DEV = ("dev_0", "dev_1", "dev_2")


epsilon = 1e-05


def from_behind(x, axis, by):
    peers = lax.axis_size(axis)
    pairs = [(i, i + by) for i in range(peers) if 0 <= i + by < peers]
    return lax.ppermute(x, axis, pairs)


def copy_for_each(x, axis):
    copies = jnp.broadcast_to(x, (lax.axis_size(axis), *x.shape))
    return lax.all_to_all(copies, axis, split_axis=0, concat_axis=0, tiled=True)


def of_everyone(x, axis):
    everything = copy_for_each(x, axis)
    return jnp.sum(everything, axis=0)


def in_one(arrays, axis):
    vector, at, finished = (jnp.concatenate([a.reshape(-1) for a in arrays]), 0, [])
    so_far = of_everyone(vector, axis)
    for a in arrays:
        finished.append(so_far[at : at + a.size].reshape(a.shape))
        at += a.size
    return tuple(finished)


def rows_for(lines, peers):
    spare = -lines.shape[0] % peers
    if not spare:
        return lines
    return jnp.concatenate([lines, jnp.zeros((spare, *lines.shape[1:]), lines.dtype)])


def laid_out(pieces, dim):
    pieces = jnp.moveaxis(pieces, 0, dim)
    shape = pieces.shape
    return pieces.reshape(*shape[:dim], shape[dim] * shape[dim + 1], *shape[dim + 2 :])


def gather_axes(x, axes, dim):
    far, near = axes
    initial = copy_for_each(x, far)
    pieces = jnp.swapaxes(copy_for_each(initial, near), 0, 1)
    return laid_out(pieces.reshape(-1, *x.shape), dim)


def split_up(x, dim, peers):
    before, after = (x.shape[:dim], x.shape[dim + 1 :])
    return jnp.moveaxis(x.reshape(*before, peers, -1, *after), dim, 0)


def summed_on_arrival(x, axis, dim):
    peers = lax.axis_size(axis)
    pieces = lax.all_to_all(split_up(x, dim, peers), axis, 0, 0, tiled=True)
    return jnp.sum(pieces, axis=0)


def sum_by_axis(x, axes, dim):
    far, near = axes
    pieces = split_up(x, dim, lax.axis_size(far))
    nearer = summed_on_arrival(pieces, near, dim + 1)
    arrived = lax.all_to_all(nearer, far, split_axis=0, concat_axis=0, tiled=True)
    return arrived.sum(axis=0)


def nested_sum(x, axes):
    padded = rows_for(x, lax.axis_size(axes[0]) * lax.axis_size(axes[1]))
    whole = gather_axes(sum_by_axis(padded, axes, 0), axes, 0)
    return lax.slice_in_dim(whole, 0, len(x)).reshape(x.shape)


def together(arrays, axis):
    vector, at, finished = (jnp.concatenate([a.reshape(-1) for a in arrays]), 0, [])
    so_far = nested_sum(vector, axis)
    for a in arrays:
        finished.append(so_far[at : at + a.size].reshape(a.shape))
        at += a.size
    return tuple(finished)


def affine(sums, squares, count, gain, shift):
    average = sums / count
    second = squares / count
    spread = gain * lax.rsqrt(second - average * average + epsilon)
    return (spread, shift - average * spread)


def silu_slope(values):
    sigma = jax.nn.sigmoid(values)
    return sigma * (1.0 + values * (1.0 - sigma))


def late_part(
    late_sent,
    entry_rows,
    gain_first,
    shift_first,
    expand_late,
    gain_inner,
    shift_inner,
    reduce_late,
):
    section_index = lax.axis_index("section")
    rows_dev = entry_rows.shape[0]
    total_rows = rows_dev * lax.axis_size(DEV)
    expand = expand_late[0]
    arrived = from_behind(late_sent[0], "section", 1)
    own_rows = jnp.where(section_index == 0, entry_rows, arrived)
    values = own_rows.astype(jnp.float32)
    sums, squares = in_one((jnp.sum(values, axis=0), jnp.sum(values * values, axis=0)), DEV)
    spread, offset = affine(sums, squares, total_rows, gain_first[0], shift_first[0])
    first = jax.nn.silu(
        lax.all_gather(own_rows, DEV, axis=0, tiled=True).astype(jnp.float32) * spread + offset
    ).astype(jnp.bfloat16)
    inner = jnp.dot(first, expand, preferred_element_type=jnp.float32)
    spread_two, offset_two = affine(
        jnp.sum(inner, axis=0),
        jnp.sum(inner * inner, axis=0),
        total_rows,
        gain_inner[0],
        shift_inner[0],
    )
    hidden = jax.nn.silu(inner * spread_two + offset_two).astype(jnp.bfloat16)
    reduce_weight = reduce_late[0]
    summed = lax.psum_scatter(
        jnp.dot(hidden, reduce_weight, preferred_element_type=jnp.float32).astype(jnp.bfloat16),
        DEV,
        scatter_dimension=0,
        tiled=True,
    ).astype(jnp.float32)
    return (own_rows.astype(jnp.float32) + summed).astype(jnp.bfloat16)[None]


def early_part(early_saved, upstream_grad, exit_grad, expand_early, reduce_early):
    section_index = lax.axis_index("section")
    arrived = from_behind(upstream_grad[0], "section", -1)
    grad = jnp.where(section_index == lax.axis_size("section") - 1, exit_grad, arrived)
    saved = early_saved[0]
    expand = expand_early[0]
    reduce_weight = reduce_early[0]
    pre = jnp.dot(saved, expand, preferred_element_type=jnp.float32)
    hidden = jax.nn.silu(pre).astype(jnp.bfloat16)
    back = lax.dot_general(
        grad, reduce_weight, (((1,), (1,)), ((), ())), preferred_element_type=jnp.float32
    )
    slope = (back * silu_slope(pre)).astype(jnp.bfloat16)
    local_expand = lax.dot_general(
        saved, slope, (((0,), (0,)), ((), ())), preferred_element_type=jnp.float32
    )
    local_reduce = lax.dot_general(
        hidden, grad, (((0,), (0,)), ((), ())), preferred_element_type=jnp.float32
    )
    summed_expand, summed_reduce = together(
        (local_expand, local_reduce), (("dev_0", "dev_1"), "dev_2")
    )
    result = grad.astype(jnp.float32) + lax.dot_general(
        slope, expand, (((1,), (1,)), ((), ())), preferred_element_type=jnp.float32
    )
    factor = 1.0 / math.sqrt(saved.shape[0] * lax.axis_size(DEV))
    return (
        result.astype(jnp.bfloat16)[None],
        (summed_expand * factor)[None],
        (summed_reduce * factor)[None],
    )


def shards(
    late_sent,
    entry_rows,
    gain_first,
    shift_first,
    expand_late,
    gain_inner,
    shift_inner,
    reduce_late,
    early_saved,
    upstream_grad,
    exit_grad,
    expand_early,
    reduce_early,
):
    late_out = late_part(
        late_sent,
        entry_rows,
        gain_first,
        shift_first,
        expand_late,
        gain_inner,
        shift_inner,
        reduce_late,
    )
    input_grad, grad_expand, grad_reduce = early_part(
        early_saved, upstream_grad, exit_grad, expand_early, reduce_early
    )
    return (late_out, input_grad, grad_expand, grad_reduce)


def solution(mesh):
    split = Mesh(
        mesh.devices.reshape(mesh.shape["section"], 2, 8, 2), ("section", "dev_0", "dev_1", "dev_2")
    )
    return jax.shard_map(
        shards,
        mesh=split,
        in_specs=(
            P("section", DEV, None),
            P(DEV, None),
            P("section", None),
            P("section", None),
            P("section", None, DEV),
            P("section", DEV),
            P("section", DEV),
            P("section", DEV, None),
            P("section", DEV, None),
            P("section", DEV, None),
            P(DEV, None),
            P("section", None, None),
            P("section", None, None),
        ),
        out_specs=(
            P("section", DEV, None),
            P("section", DEV, None),
            P("section", None, None),
            P("section", None, None),
        ),
        check_vma=False,
    )
```

profile of v0, /device:TPU:12, one launch (start us, length us, event | category | flops | bytes accessed | tf_op | source)
XLA Modules:
  0.0 298.4 jit_solution(14696749098420810229)
XLA Ops:
  7.2 3.2 %collective-permute-start = (bf16[98,1024]{1,0:T(8,128)(2,1)}, bf16[98,1024]{1,0:T(8,128)(2,1)S(1)}, u32[]{:S(2)}, u32[]{:S(2)}) collective-permute-start(bf16[98,1024]{1,0:T(8,128)(2,1)} %bitcast.74), channel_id=1, source_target_pairs={{0,32},{32,64},{64,96},{96,128},{128,160},{160,192},{192,224},{1,3... | collective-permute-start | bytes 602120 | tf_op jit(solution)/shard_map/ppermute | solution.py:18
  10.5 6.9 %collective-permute-done = bf16[98,1024]{1,0:T(8,128)(2,1)S(1)} collective-permute-done((bf16[98,1024]{1,0:T(8,128)(2,1)}, bf16[98,1024]{1,0:T(8,128)(2,1)S(1)}, u32[]{:S(2)}, u32[]{:S(2)}) %collective-permute-start) | collective-permute-done | bytes 200736 | tf_op jit(solution)/shard_map/ppermute | solution.py:18
  17.4 0.8 convert_reduce_fusion
  18.2 2.1 collective-permute-start.1
  20.3 2.1 fusion.5
  22.4 18.9 %collective-permute-done.1 = bf16[1568,256]{1,0:T(8,128)(2,1)S(1)} collective-permute-done((bf16[1568,256]{1,0:T(8,128)(2,1)}, bf16[1568,256]{1,0:T(8,128)(2,1)S(1)}, u32[]{:S(2)}, u32[]{:S(2)}) %collective-permute-start.1) | collective-permute-done | bytes 802848 | tf_op jit(solution)/shard_map/ppermute | solution.py:18
  41.4 2.8 multiply_convert_fusion.2
  44.2 1.7 copy-done.16
  46.0 1.2 convolution_bitcast_fusion
  47.1 0.3 copy.29
  47.5 0.9 concatenate.12
  48.4 5.9 %fusion.2 = f32[1024,256]{1,0:T(8,128)} fusion(bf16[1568,256]{1,0:T(8,128)(2,1)} %copy-done.5, f32[1568,1024]{1,0:T(8,128)} %copy-done.2), kind=kOutput, calls=%fused_computation.6 | convolution fusion | flops 830111744 | bytes 8273920 | tf_op jit(solution)/shard_map/dot_general | solution.py:163
  54.2 1.9 concatenate.13
  56.2 1.0 maximum_bitcast_fusion
  57.2 1.2 copy.30
  58.4 5.4 %all_to_all.34 = f32[2,16,16384]{2,1,0:T(8,128)S(1)} all-to-all(f32[2,16,16384]{2,1,0:T(8,128)S(1)} %copy.30), channel_id=1, replica_groups=mesh['section'=8,'dev_0'=2,'dev_1'=8,'dev_2'=2] {'dev_2'}, dimensions={0} | all-to-all | bytes 4194304 | tf_op jit(solution)/shard_map/all_to_all | solution.py:67
  63.9 1.2 reduce_sum.68
  65.1 3.3 %all_to_all.24 = f32[16,1,16384]{2,1,0:T(1,128)} reshape(f32[16,16384]{1,0:T(8,128)} %reduce_sum.68) | data formatting | bytes 2097152 | tf_op jit(solution)/shard_map/all_to_all | solution.py:75
  68.4 11.5 %all-to-all-start.2 = ((f32[16,1,16384]{2,1,0:T(1,128)}), f32[16,1,16384]{2,1,0:T(1,128)S(1)}, u32[]{:S(2)}, u32[]{:S(2)}) async-start(f32[16,1,16384]{2,1,0:T(1,128)} %all_to_all.24), calls=%async_computation.2 | async-start | bytes 2097152 | tf_op jit(solution)/shard_map/all_to_all | solution.py:75
  79.9 29.3 %all-to-all-done.2 = f32[16,1,16384]{2,1,0:T(1,128)S(1)} async-done(((f32[16,1,16384]{2,1,0:T(1,128)}), f32[16,1,16384]{2,1,0:T(1,128)S(1)}, u32[]{:S(2)}, u32[]{:S(2)}) %all-to-all-start.2) | async-done | bytes 1048608 | tf_op jit(solution)/shard_map/all_to_all | solution.py:75
  109.1 0.8 broadcast_in_dim.10
  109.9 7.7 %all-to-all-start = ((f32[32,1,2048]{2,1,0:T(1,128)}), f32[32,1,2048]{2,1,0:T(1,128)S(1)}, u32[]{:S(2)}, u32[]{:S(2)}) async-start(f32[32,1,2048]{2,1,0:T(1,128)} %broadcast_in_dim.10), calls=%async_computation | async-start | bytes 524288 | tf_op jit(solution)/shard_map/all_to_all | solution.py:23
  117.7 0.7 reduce_sum.69
  118.4 10.9 %all-to-all-done = f32[32,1,2048]{2,1,0:T(1,128)S(1)} async-done(((f32[32,1,2048]{2,1,0:T(1,128)}), f32[32,1,2048]{2,1,0:T(1,128)S(1)}, u32[]{:S(2)}, u32[]{:S(2)}) %all-to-all-start) | async-done | bytes 262176 | tf_op jit(solution)/shard_map/all_to_all | solution.py:23
  129.3 1.8 broadcast_in_dim.24
  131.0 7.2 %all-to-all-start.3 = ((f32[16,1,16384]{2,1,0:T(1,128)}), f32[16,1,16384]{2,1,0:T(1,128)S(1)}, u32[]{:S(2)}, u32[]{:S(2)}) async-start(f32[16,1,16384]{2,1,0:T(1,128)} %broadcast_in_dim.24), calls=%async_computation.3 | async-start | bytes 2097152 | tf_op jit(solution)/shard_map/all_to_all | solution.py:23
  138.2 0.6 dynamic-slice.4
  139.4 0.2 reduce_sum.65
  139.7 3.8 %fusion.3 = bf16[1,1568,256]{2,1,0:T(8,128)(2,1)} fusion(bf16[1568,256]{1,0:T(8,128)(2,1)S(1)} %copy-done.6, bf16[1568,1024]{1,0:T(8,128)(2,1)} %copy-done.16, bf16[1,256,1024]{2,1,0:T(8,128)(2,1)S(1)} %copy-done.7), kind=kOutput, calls=%fused_computation.15 | convolution fusion | flops 823287808 | bytes 5341184 | tf_op jit(solution)/shard_map/dot_general | solution.py:169
  143.5 20.7 %all-to-all-done.3 = f32[16,1,16384]{2,1,0:T(1,128)S(1)} async-done(((f32[16,1,16384]{2,1,0:T(1,128)}), f32[16,1,16384]{2,1,0:T(1,128)S(1)}, u32[]{:S(2)}, u32[]{:S(2)}) %all-to-all-start.3) | async-done | bytes 1048608 | tf_op jit(solution)/shard_map/all_to_all | solution.py:23
  164.3 0.6 copy.38
  164.9 1.5 broadcast_in_dim.25
  166.4 3.8 %all-to-all-start.4 = ((f32[2,16,16384]{2,1,0:T(8,128)}), f32[2,16,16384]{2,1,0:T(8,128)S(1)}, u32[]{:S(2)}, u32[]{:S(2)}) async-start(f32[2,16,16384]{2,1,0:T(8,128)} %broadcast_in_dim.25), calls=%async_computation.4 | async-start | bytes 4194304 | tf_op jit(solution)/shard_map/all_to_all | solution.py:23
  170.2 9.4 %reshape.93 = f32[3136,1024]{1,0:T(8,128)} reshape(bf16[32,98,1024]{2,1,0:T(8,128)(2,1)} %all-gather.3.cloned.1.call-done) | data formatting | bytes 19267584 | tf_op jit(solution)/shard_map/convert_element_type | solution.py:126
  179.6 6.8 %fusion.31 = (f32[128]{0:T(128)S(1)}, f32[128]{0:T(128)S(1)}, f32[3136,128]{1,0:T(8,128)S(1)}) fusion(bf16[1,1024,128]{2,1,0:T(8,128)(2,1)S(1)} %copy-done.14, f32[3136,1024]{1,0:T(8,128)} %reshape.93, f32[1024]{0:T(1024)S(1)} %get-tuple-element.10, f32[1024]{0:T(1024)S(1)} %get-tuple-element.11), kind=kOutput, calls=%fused_computation.53 | convolution fusion | flops 845766400 | bytes 14722048 | tf_op jit(solution)/shard_map/dot_general | solution.py:128
  186.4 4.5 %convolution_convert_fusion = bf16[3136,1024]{1,0:T(8,128)(2,1)} fusion(f32[3136,128]{1,0:T(8,128)S(1)} %get-tuple-element.15, f32[128]{0:T(128)S(1)} %get-tuple-element.8, f32[128]{0:T(128)S(1)} %bitcast.72, bf16[1,128,1024]{2,1,0:T(8,128)(2,1)S(1)} %copy-done.15), kind=kOutput, calls=%fused_computation.1 | convolution fusion | flops 828104704 | bytes 8291328 | tf_op jit(solution)/shard_map/dot_general | solution.py:139
  191.0 82.9 %fusion = bf16[104,1024]{1,0:T(8,128)(2,1)S(1)} fusion(bf16[3136,1024]{1,0:T(8,128)(2,1)} %convolution_convert_fusion), kind=kCustom, calls=%all-reduce-scatter | all-reduce-scatter fusion | flops 3407873 | bytes 6636544
  273.8 0.7 slice.22
  274.5 1.9 collective-permute-start.2
  276.5 2.1 collective-permute-start.3
  278.6 1.2 slice_multiply_fusion
  279.8 0.8 copy.31
  280.6 1.9 mul.125
  282.5 2.0 copy.32
  284.5 1.9 mul.127
  286.4 2.9 collective-permute-done.3
  289.3 1.5 concatenate.15
  290.8 0.8 fusion.20
  (42 shorter events, 0.3 us)
Async XLA Ops:
  7.2 13.1 %copy-start = (bf16[1,1568,256]{2,1,0:T(8,128)(2,1)S(1)}, bf16[1,1568,256]{2,1,0:T(8,128)(2,1)}, u32[]{:S(2)}) copy-start(bf16[1,1568,256]{2,1,0:T(8,128)(2,1)} %param.21) | copy-start | bytes 2408452
  7.2 34.2 %copy-start.4 = (bf16[1568,256]{1,0:T(8,128)(2,1)S(1)}, bf16[1568,256]{1,0:T(8,128)(2,1)}, u32[]{:S(2)}) copy-start(bf16[1568,256]{1,0:T(8,128)(2,1)} %param.23) | copy-start | bytes 2408452
  7.2 163.0 %all-gather.3.cloned.1.call-start = ((), (), s32[]{:S(2)}) async-start(), calls=%async_computation.5 | async-start | bytes 7028736 | tf_op jit(solution)/shard_map/all_gather | solution.py:126
  7.2 10.1 %collective-permute-start = (bf16[98,1024]{1,0:T(8,128)(2,1)}, bf16[98,1024]{1,0:T(8,128)(2,1)S(1)}, u32[]{:S(2)}, u32[]{:S(2)}) collective-permute-start(bf16[98,1024]{1,0:T(8,128)(2,1)} %bitcast.74), channel_id=1, source_target_pairs={{0,32},{32,64},{64,96},{96,128},{128,160},{160,192},{192,224},{1,3... | collective-permute-start | bytes 602120 | tf_op jit(solution)/shard_map/ppermute | solution.py:18
  18.2 23.2 %collective-permute-start.1 = (bf16[1568,256]{1,0:T(8,128)(2,1)}, bf16[1568,256]{1,0:T(8,128)(2,1)S(1)}, u32[]{:S(2)}, u32[]{:S(2)}) collective-permute-start(bf16[1568,256]{1,0:T(8,128)(2,1)} %bitcast.73), channel_id=1, source_target_pairs={{32,0},{64,32},{96,64},{128,96},{160,128},{192,160},{224,192},{33,... | collective-permute-start | bytes 2408456 | tf_op jit(solution)/shard_map/ppermute | solution.py:18
  20.3 21.1 %copy-start.13 = (bf16[1,1024,256]{2,1,0:T(8,128)(2,1)S(1)}, bf16[1,1024,256]{2,1,0:T(8,128)(2,1)}, u32[]{:S(2)}) copy-start(bf16[1,1024,256]{2,1,0:T(8,128)(2,1)} %param.25) | copy-start | bytes 1572868
  22.4 21.8 %copy-start.2 = (f32[1568,1024]{1,0:T(8,128)}, f32[1568,1024]{1,0:T(8,128)S(1)}, u32[]{:S(2)}) copy-start(f32[1568,1024]{1,0:T(8,128)S(1)} %fusion.5) | copy-start | bytes 19267588
  41.4 2.8 copy-start.5
  44.2 1.8 copy-start.16
  63.8 74.4 %copy-start.12 = (u32[256]{0:T(256)S(1)}, u32[256]{0:T(256)}, u32[]{:S(2)}) copy-start(u32[256]{0:T(256)} %constant.47) | copy-start | bytes 3076
  63.8 75.8 %copy-start.8 = (f32[1,1024]{1,0:T(1,128)S(1)}, f32[1,1024]{1,0:T(1,128)}, u32[]{:S(2)}) copy-start(f32[1,1024]{1,0:T(1,128)} %param.16) | copy-start | bytes 12292
  63.8 75.8 %copy-start.9 = (f32[1,1024]{1,0:T(1,128)S(1)}, f32[1,1024]{1,0:T(1,128)}, u32[]{:S(2)}) copy-start(f32[1,1024]{1,0:T(1,128)} %param.15) | copy-start | bytes 12292
  63.8 75.8 %copy-start.7 = (bf16[1,256,1024]{2,1,0:T(8,128)(2,1)S(1)}, bf16[1,256,1024]{2,1,0:T(8,128)(2,1)}, u32[]{:S(2)}) copy-start(bf16[1,256,1024]{2,1,0:T(8,128)(2,1)} %param.24) | copy-start | bytes 1572868
  65.0 74.6 %copy-start.6 = (bf16[1568,256]{1,0:T(8,128)(2,1)S(1)}, bf16[1568,256]{1,0:T(8,128)(2,1)}, u32[]{:S(2)}) copy-start(bf16[1568,256]{1,0:T(8,128)(2,1)} %copy-done.5) | copy-start | bytes 2408452
  68.4 40.7 %all-to-all-start.2 = ((f32[16,1,16384]{2,1,0:T(1,128)}), f32[16,1,16384]{2,1,0:T(1,128)S(1)}, u32[]{:S(2)}, u32[]{:S(2)}) async-start(f32[16,1,16384]{2,1,0:T(1,128)} %all_to_all.24), calls=%async_computation.2 | async-start | bytes 2097152 | tf_op jit(solution)/shard_map/all_to_all | solution.py:75
  109.9 19.3 %all-to-all-start = ((f32[32,1,2048]{2,1,0:T(1,128)}), f32[32,1,2048]{2,1,0:T(1,128)S(1)}, u32[]{:S(2)}, u32[]{:S(2)}) async-start(f32[32,1,2048]{2,1,0:T(1,128)} %broadcast_in_dim.10), calls=%async_computation | async-start | bytes 524288 | tf_op jit(solution)/shard_map/all_to_all | solution.py:23
  131.0 33.2 %all-to-all-start.3 = ((f32[16,1,16384]{2,1,0:T(1,128)}), f32[16,1,16384]{2,1,0:T(1,128)S(1)}, u32[]{:S(2)}, u32[]{:S(2)}) async-start(f32[16,1,16384]{2,1,0:T(1,128)} %broadcast_in_dim.24), calls=%async_computation.3 | async-start | bytes 2097152 | tf_op jit(solution)/shard_map/all_to_all | solution.py:23
  166.4 112.2 %all-to-all-start.4 = ((f32[2,16,16384]{2,1,0:T(8,128)}), f32[2,16,16384]{2,1,0:T(8,128)S(1)}, u32[]{:S(2)}, u32[]{:S(2)}) async-start(f32[2,16,16384]{2,1,0:T(8,128)} %broadcast_in_dim.25), calls=%async_computation.4 | async-start | bytes 4194304 | tf_op jit(solution)/shard_map/all_to_all | solution.py:23
  170.1 9.4 %copy-start.14 = (bf16[1,1024,128]{2,1,0:T(8,128)(2,1)S(1)}, bf16[1,1024,128]{2,1,0:T(8,128)(2,1)}, u32[]{:S(2)}) copy-start(bf16[1,1024,128]{2,1,0:T(8,128)(2,1)} %param.17) | copy-start | bytes 786436
  179.5 6.8 %copy-start.10 = (f32[1,128]{1,0:T(1,128)S(1)}, f32[1,128]{1,0:T(1,128)}, u32[]{:S(2)}) copy-start(f32[1,128]{1,0:T(1,128)} %param.19) | copy-start | bytes 1540
  179.5 6.8 %copy-start.11 = (f32[1,128]{1,0:T(1,128)S(1)}, f32[1,128]{1,0:T(1,128)}, u32[]{:S(2)}) copy-start(f32[1,128]{1,0:T(1,128)} %param.18) | copy-start | bytes 1540
  179.6 6.9 %copy-start.15 = (bf16[1,128,1024]{2,1,0:T(8,128)(2,1)S(1)}, bf16[1,128,1024]{2,1,0:T(8,128)(2,1)}, u32[]{:S(2)}) copy-start(bf16[1,128,1024]{2,1,0:T(8,128)(2,1)} %param.20) | copy-start | bytes 786436
  274.5 14.7 %collective-permute-start.2 = (bf16[104,1024]{1,0:T(8,128)(2,1)S(1)}, bf16[104,1024]{1,0:T(8,128)(2,1)S(1)}, u32[]{:S(2)}, u32[]{:S(2)}) collective-permute-start(bf16[104,1024]{1,0:T(8,128)(2,1)S(1)} %fusion), channel_id=1, source_target_pairs={{0,1},{1,2},{2,3},{3,4},{4,5},{5,6},{6,7},{7,8},{8,9},{9,10},{10,1... | collective-permute-start | bytes 638984
  276.5 12.8 %collective-permute-start.3 = (bf16[82,1024]{1,0:T(8,128)(2,1)}, bf16[82,1024]{1,0:T(8,128)(2,1)}, u32[]{:S(2)}, u32[]{:S(2)}) collective-permute-start(bf16[82,1024]{1,0:T(8,128)(2,1)} %slice.22), channel_id=1, source_target_pairs={{0,2},{1,3},{2,4},{3,5},{4,6},{5,7},{6,8},{7,9},{8,10},{9,11},{10,... | collective-permute-start | bytes 503816
  278.6 12.9 %copy-start.1 = (bf16[1,1568,256]{2,1,0:T(8,128)(2,1)S(1)}, bf16[1,1568,256]{2,1,0:T(8,128)(2,1)}, u32[]{:S(2)}) copy-start(bf16[1,1568,256]{2,1,0:T(8,128)(2,1)} %param.21) | copy-start | bytes 2408452
  278.6 12.2 %copy-start.3 = (bf16[98,1024]{1,0:T(8,128)(2,1)S(1)}, bf16[98,1024]{1,0:T(8,128)(2,1)}, u32[]{:S(2)}) copy-start(bf16[98,1024]{1,0:T(8,128)(2,1)} %get-tuple-element.12) | copy-start | bytes 602116
Sparse Core Ops, SparseCore 0:
  18.3 111.2 all-gather.2
where the time goes:
time: 299 us; the launch traced here: 298 us
  waiting for transfers between devices  89.6 us (30%)
  blocking collectives  88.3 us (30%)
  starting transfers between devices  39.5 us (13%)
  local copies, waits for them, and re-layouts  33 us (11%)
  matrix products  27 us (9%)
  between operations  15.1 us (5%)
  other arithmetic  5.88 us (2%)
    unnamed x1, blocking collectives  82.9 us
    all_to_all x3, waiting for transfers between devices, copy_for_each(): return lax.all_to_all(copies, axis, split_axis=0, concat_axis=0, tiled=True)  31.7 us
    all_to_all x1, waiting for transfers between devices, sum_by_axis(): lax.all_to_all(nearer, far, split_axis=0, concat_axis=0, tiled=True)  29.3 us
    ppermute x2, waiting for transfers between devices, from_behind(): return lax.ppermute(x, axis, pairs)  25.8 us
    all_to_all x3, starting transfers between devices, copy_for_each(): return lax.all_to_all(copies, axis, split_axis=0, concat_axis=0, tiled=True)  18.6 us
    all_to_all x1, starting transfers between devices, sum_by_axis(): lax.all_to_all(nearer, far, split_axis=0, concat_axis=0, tiled=True)  11.5 us
    convert_element_type x1, local copies, waits for them, and re-layouts, late_part(): lax.all_gather(own_rows, DEV, axis=0, tiled=True).astype(jnp.float32)  9.37 us
    dot_general x1, matrix products, late_part(): inner = jnp.dot(first, expand, preferred_element_type=jnp.float32)  6.79 us
  transfers between devices with their start and end apart: 9, of which 6 were waited for; matrix products, arithmetic and copies ran while one was open for 47% of the time, Pallas kernels for 0%

commit v1 on v0

v1 whole, which is shorter than its diff:
```python
import functools
import math

import jax
import jax.numpy as jnp
from jax import lax
from jax.experimental import pallas as pl
from jax.experimental.pallas import tpu as pltpu
from jax.sharding import Mesh
from jax.sharding import PartitionSpec as P

DEV = ("b", "z", "c")
MESH = pl.DeviceIdType.MESH
F32 = jnp.float32
BF16 = jnp.bfloat16
EPS = 1e-05
Q = 4
PIECES = 7
BLOCK = 256
N_SEMS = 320


def silu(v):
    return v * jax.nn.sigmoid(v)


def affine(sums, squares, count, gain, shift):
    average = sums / count
    second = squares / count
    spread = gain * lax.rsqrt(second - average * average + EPS)
    return spread, shift - average * spread


def kernel(
    sizes,
    late_ref,
    entry_ref,
    gain_first_ref,
    shift_first_ref,
    expand_late_ref,
    gain_inner_ref,
    shift_inner_ref,
    reduce_late_ref,
    saved_ref,
    up_ref,
    exit_ref,
    expand_early_ref,
    reduce_early_ref,
    late_out_ref,
    input_grad_ref,
    grads_ref,
    S,
    ZST,
    ZT,
    FST,
    GS,
    G,
    F,
    W1,
    W2,
    GI,
    SI,
    IST,
    INN,
    PT,
    SC,
    SA,
    RC,
    RA,
    LO,
    SV,
    GR,
    WE1,
    WE2,
    ACT,
    DS,
    OG,
    ACC,
    SD,
    RD,
    SX,
    RX,
    TF,
    SZ,
    RZ,
    FIN,
    sems,
):
    NS, NZ = sizes
    H = NZ // 2
    rows, CL = S.shape
    CQ = CL // Q
    HID = expand_late_ref.shape[1]
    e_rows, CE = SV.shape
    FE = WE1.shape[1]
    PR = e_rows // PIECES
    ZR = CE // 2 // NZ
    late_count = rows * NZ * 4

    s = lax.axis_index("section")
    b = lax.axis_index("b")
    z = lax.axis_index("z")
    c = lax.axis_index("c")
    ahead = lax.rem(s + 1, NS)
    behind = lax.rem(s + NS - 1, NS)
    other_b = 1 - b
    other_c = 1 - c

    def zat(d):
        return lax.rem(z + d + NZ, NZ)

    def group(k):
        where = {}
        if k & 2:
            where["b"] = other_b
        if k & 1:
            where["c"] = other_c
        return where

    used = [0]
    sent = []

    def new_sem():
        used[0] += 1
        return sems.at[used[0] - 1]

    def remote(src, dst, to, pair=None):
        pair = pair or (new_sem(), new_sem())
        return pltpu.make_async_remote_copy(
            src_ref=src, dst_ref=dst, send_sem=pair[0], recv_sem=pair[1], device_id=to, device_id_type=MESH
        )

    def send(src, dst, to):
        copy = remote(src, dst, to)
        copy.start()
        sent.append(copy)
        return copy

    def send_either(condition, one, two, dst, to):
        pair = (new_sem(), new_sem())
        first, second = remote(one, dst, to, pair), remote(two, dst, to, pair)

        @pl.when(condition)
        def _():
            first.start()

        @pl.when(jnp.logical_not(condition))
        def _():
            second.start()

        sent.append(first)
        return first

    def load(src, dst):
        copy = pltpu.make_async_copy(src, dst, new_sem())
        copy.start()
        return copy

    def cols(q):
        return slice(q * CQ, (q + 1) * CQ)

    barrier = pltpu.get_barrier_semaphore()
    greeted = [{"z": zat(d)} for d in range(1, NZ)] + [group(k) for k in (1, 2, 3)]
    greeted += [{"section": ahead, **group(k)} for k in range(4)]
    greeted += [{"section": behind, **group(k)} for k in range(4)]
    for to in greeted:
        pl.semaphore_signal(barrier, inc=1, device_id=to, device_id_type=MESH)

    last = s == NS - 1
    sem_s = new_sem()
    take_late = pltpu.make_async_copy(late_ref, S, sem_s)
    take_entry = pltpu.make_async_copy(entry_ref, S, sem_s)

    @pl.when(last)
    def _():
        take_entry.start()

    @pl.when(jnp.logical_not(last))
    def _():
        take_late.start()

    load_saved = load(saved_ref, SV)
    load_we1 = load(expand_early_ref, WE1)
    load_we2 = load(reduce_early_ref, WE2)
    load_gf = load(gain_first_ref, GS.at[0])
    load_sf = load(shift_first_ref, GS.at[1])
    load_w1 = load(expand_late_ref, W1.at[:, 0:HID])
    load_w2 = load(reduce_late_ref, W2.at[0:HID, :])
    load_gi = load(gain_inner_ref, GI.at[0])
    load_si = load(shift_inner_ref, SI.at[0])

    take_late.wait()
    for q in range(Q):
        values = S[:, cols(q)].astype(F32)
        ZST[0, 0:1, cols(q)] = jnp.sum(values, axis=0, keepdims=True)
        ZST[0, 1:2, cols(q)] = jnp.sum(values * values, axis=0, keepdims=True)

    pl.semaphore_wait(barrier, len(greeted))

    shift_late = [
        send_either(last, entry_ref.at[:, cols(q)], late_ref.at[:, cols(q)], G.at[0, :, cols(q)], {"section": ahead})
        for q in range(Q)
    ]
    z_stats = [send(ZST.at[0], ZST.at[d], {"z": zat(d)}) for d in range(1, NZ)]

    w1_near = send(expand_late_ref, W1.at[:, HID : 2 * HID], group(1))
    w1_far = send(expand_late_ref, W1.at[:, 2 * HID : 3 * HID], group(2))
    gains = []
    for k in (1, 2, 3):
        gains.append(send(gain_inner_ref, GI.at[k], group(k)))
        gains.append(send(shift_inner_ref, SI.at[k], group(k)))

    grad_pairs = [(new_sem(), new_sem()) for _ in range(PIECES)]
    first_grad = s == 0
    for p in range(PIECES):
        piece = slice(p * PR, (p + 1) * PR)
        one = remote(exit_ref.at[piece], GR.at[piece], {"section": behind}, grad_pairs[p])
        two = remote(up_ref.at[piece], GR.at[piece], {"section": behind}, grad_pairs[p])
        pl.when(first_grad)(one.start)
        pl.when(jnp.logical_not(first_grad))(two.start)
        sent.append(two)
    shift_grad = sent[-PIECES:]

    w2_near = send(reduce_late_ref, W2.at[HID : 2 * HID, :], group(1))
    w2_far = send(reduce_late_ref, W2.at[2 * HID : 3 * HID, :], group(2))

    load_saved.wait()
    load_we1.wait()
    load_we2.wait()

    def early_rows(p):
        return pl.ds(pl.multiple_of(p * PR, PR), PR)

    def early_one(p, carry):
        at = early_rows(p)
        saved = SV[at, :]
        for f in range(0, FE, BLOCK):
            pre = jnp.dot(saved, WE1[:, f : f + BLOCK], preferred_element_type=F32)
            sigma = jax.nn.sigmoid(pre)
            ACT[at, f : f + BLOCK] = (pre * sigma).astype(BF16)
            DS[at, f : f + BLOCK] = sigma * (1.0 + pre * (1.0 - sigma))
        return carry

    lax.fori_loop(0, PIECES, early_one, 0)

    ACC[...] = jnp.zeros(ACC.shape, F32)

    def early_two(p):
        at = slice(p * PR, (p + 1) * PR)
        shift_grad[p].wait_recv()
        grad = GR[at, :]
        saved = SV[at, :]
        result = grad.astype(F32)
        for f in range(0, FE, BLOCK):
            block = slice(f, f + BLOCK)
            back = lax.dot_general(grad, WE2[block, :], (((1,), (1,)), ((), ())), preferred_element_type=F32)
            slope = (back * DS[at, block]).astype(BF16)
            ACC[0, :, block] += lax.dot_general(saved, slope, (((0,), (0,)), ((), ())), preferred_element_type=F32)
            ACC[1, :, block] += lax.dot_general(
                grad, ACT[at, block], (((0,), (0,)), ((), ())), preferred_element_type=F32
            )
            result += lax.dot_general(slope, WE1[:, block], (((1,), (1,)), ((), ())), preferred_element_type=F32)
        OG[at, :] = result.astype(BF16)
        return load(OG.at[at], input_grad_ref.at[at])

    hops_c, hops_a = [], []

    def forward(t, q):
        if t < H or q < Q // 2:
            hops_c.append((t, q, send(G.at[t - 1, :, cols(q)], G.at[t, :, cols(q)], {"z": zat(1)})))
        if t < H or q >= Q // 2:
            src, dst = (NZ - t + 1) % NZ, NZ - t
            hops_a.append((t, q, send(G.at[src, :, cols(q)], G.at[dst, :, cols(q)], {"z": zat(-1)})))

    def arrived(t, q):
        for hops in (hops_c, hops_a):
            for u, r, copy in hops:
                if (u, r) == (t, q):
                    copy.wait_recv()

    for q in range(Q):
        shift_late[q].wait_recv()
        forward(1, q)

    for copy in z_stats:
        copy.wait_recv()
    total = ZST[0]
    for d in range(1, NZ):
        total = total + ZST[d]
    ZT[...] = total
    first_stats = [send(ZT, FST.at[k], {"section": ahead, **group(k)}) for k in range(4)]

    if H > 1:
        for q in range(Q):
            arrived(1, q)
            forward(2, q)

    for copy in first_stats:
        copy.wait_recv()
    load_gf.wait()
    load_sf.wait()
    sums = FST[0] + FST[1] + FST[2] + FST[3]
    spread, offset = affine(sums[0:1], sums[1:2], late_count, GS[0], GS[1])

    def first_of(slot):
        for q in range(Q):
            at = cols(q)
            values = G[slot, :, at].astype(F32) * spread[:, at] + offset[:, at]
            F[slot, :, at] = silu(values).astype(BF16)

    stats = [0.0, 0.0]

    def inner_of(slot):
        inner = jnp.dot(F[slot], W1[...], preferred_element_type=F32)
        INN[slot] = inner
        stats[0] += jnp.sum(inner, axis=0, keepdims=True)
        stats[1] += jnp.sum(inner * inner, axis=0, keepdims=True)

    first_of(0)
    done = []
    for t in range(2, H):
        for q in range(Q):
            arrived(t, q)
            forward(t + 1, q)
        for slot in (t - 1, NZ - t + 1):
            first_of(slot)
            done.append(slot)

    w1_far.wait_recv()
    w1_fwd = send(W1.at[:, 2 * HID : 3 * HID], W1.at[:, 3 * HID :], group(1))
    load_w1.wait()
    w1_near.wait_recv()
    w1_fwd.wait_recv()
    for slot in [0] + done:
        inner_of(slot)
    for slot in (H - 1, H + 1):
        if slot not in done and slot != 0 and H > 1:
            first_of(slot)
            inner_of(slot)
    for q in range(Q):
        arrived(H, q)
    first_of(H)
    inner_of(H)

    IST[0, 0:1] = stats[0]
    IST[0, 1:2] = stats[1]
    inner_stats = [send(IST.at[0], IST.at[k], group(k)) for k in (1, 2, 3)]

    out_grads = []
    for p in range(PIECES // 2):
        out_grads.append(early_two(p))

    w2_far.wait_recv()
    w2_fwd = send(W2.at[2 * HID : 3 * HID, :], W2.at[3 * HID :, :], group(1))
    load_w2.wait()
    load_gi.wait()
    load_si.wait()
    w2_near.wait_recv()
    for copy in gains:
        copy.wait_recv()
    for copy in inner_stats:
        copy.wait_recv()
    spreads, offsets = [], []
    for k in range(4):
        piece = IST[0, :, k * HID : (k + 1) * HID]
        for d in (1, 2, 3):
            j = k ^ d
            piece = piece + IST[d, :, j * HID : (j + 1) * HID]
        one, two = affine(piece[0:1], piece[1:2], late_count, GI[k], SI[k])
        spreads.append(one)
        offsets.append(two)
    spread_two = jnp.concatenate(spreads, axis=1)
    offset_two = jnp.concatenate(offsets, axis=1)
    w2_fwd.wait_recv()

    def partial_of(slot):
        hidden = silu(INN[slot] * spread_two + offset_two).astype(BF16)
        PT[slot] = jnp.dot(hidden, W2[...], preferred_element_type=F32)

    sums_c, sums_a = {}, {}

    def sum_hop(t):
        for q in range(Q):
            at = cols(q)
            for slot, sums_d, S_, R_, step, half in (
                (NZ - (H - t), sums_c, SC, RC, 1, q < Q // 2),
                (H - t, sums_a, SA, RA, -1, q >= Q // 2),
            ):
                if t == 0 and not half:
                    continue
                value = PT[slot, :, at]
                if t > 1 or (t == 1 and half):
                    sums_d[t - 1, q].wait_recv()
                    value = value + R_[t - 1, :, at].astype(F32)
                S_[t, :, at] = value.astype(BF16)
                sums_d[t, q] = send(S_.at[t, :, at], R_.at[t, :, at], {"z": zat(step)})

    partial_of(H)
    sum_hop(0)
    for t in range(1, H):
        partial_of(NZ - (H - t))
        partial_of(H - t)
        sum_hop(t)
        if t == 1:
            for p in range(PIECES // 2, PIECES):
                out_grads.append(early_two(p))
            for half in (0, 1):
                h = other_b if half == 0 else b
                at = pl.ds(pl.multiple_of(h * (CE // 2), CE // 2), CE // 2)
                SD[h] = ACC[other_c, at, :].astype(BF16)
            pair_sums = [send(SD.at[h], RD.at[h], group(1)) for h in (other_b, b)]
    partial_of(0)

    half_other = pl.ds(pl.multiple_of(other_b * (CE // 2), CE // 2), CE // 2)
    half_own = pl.ds(pl.multiple_of(b * (CE // 2), CE // 2), CE // 2)
    pair_sums[0].wait_recv()
    pair_sums[1].wait_recv()
    SX[...] = (ACC[c, half_other, :] + RD[other_b].astype(F32)).astype(BF16)
    x_sum = send(SX, RX, group(2))

    for q in range(Q):
        at = cols(q)
        if H > 1 or q < Q // 2:
            sums_c[H - 1, q].wait_recv()
        if H > 1 or q >= Q // 2:
            sums_a[H - 1, q].wait_recv()
        value = PT[0, :, at]
        if H > 1 or q < Q // 2:
            value = value + RC[H - 1, :, at].astype(F32)
        if H > 1 or q >= Q // 2:
            value = value + RA[H - 1, :, at].astype(F32)
        LO[:, at] = (G[0, :, at].astype(F32) + value).astype(BF16)
    out_late = load(LO, late_out_ref)

    x_sum.wait_recv()
    TF[...] = ACC[c, half_own, :] + RD[b].astype(F32) + RX[...].astype(F32)
    SZ[...] = TF[...].astype(BF16)

    def zrows(i):
        return pl.ds(pl.multiple_of(i * ZR, ZR), ZR)

    z_sums = [send(SZ.at[zrows(zat(d))], RZ.at[d], {"z": zat(d)}) for d in range(1, NZ)]
    value = TF[zrows(z), :]
    for d, copy in enumerate(z_sums, 1):
        copy.wait_recv()
        value = value + RZ[d].astype(F32)
    factor = 1.0 / math.sqrt(e_rows * NZ * 4)
    FIN[c, b, zrows(z), :] = (value * factor).astype(BF16)
    own = FIN.at[c, b, zrows(z)]
    z_back = [send(own, own, {"z": zat(d)}) for d in range(1, NZ)]
    for copy in z_back:
        copy.wait_recv()
    x_back = send(FIN.at[c, b], FIN.at[c, b], group(2))
    c_back = send(FIN.at[c, b], FIN.at[c, b], group(1))
    x_back.wait_recv()
    c_back_two = send(FIN.at[c, other_b], FIN.at[c, other_b], group(1))
    c_back.wait_recv()
    c_back_two.wait_recv()
    out_fin = load(FIN, grads_ref)

    for copy in sent:
        copy.wait_send()
    for copy in out_grads:
        copy.wait()
    out_late.wait()
    out_fin.wait()


def shards(
    late_sent,
    entry_rows,
    gain_first,
    shift_first,
    expand_late,
    gain_inner,
    shift_inner,
    reduce_late,
    early_saved,
    upstream_grad,
    exit_grad,
    expand_early,
    reduce_early,
):
    rows, CL = entry_rows.shape
    e_rows, CE = exit_grad.shape
    FE = expand_early.shape[2]
    HID = expand_late.shape[2]
    NS, NZ = lax.axis_size("section"), lax.axis_size("z")
    H = NZ // 2
    VM = pltpu.VMEM
    scratch = [
        VM((rows, CL), BF16),
        VM((NZ, 2, CL), F32),
        VM((2, CL), F32),
        VM((4, 2, CL), F32),
        VM((2, 1, CL), F32),
        VM((NZ, rows, CL), BF16),
        VM((NZ, rows, CL), BF16),
        VM((CL, 4 * HID), BF16),
        VM((4 * HID, CL), BF16),
        VM((4, 1, HID), F32),
        VM((4, 1, HID), F32),
        VM((4, 2, 4 * HID), F32),
        VM((NZ, rows, 4 * HID), F32),
        VM((NZ, rows, CL), F32),
        VM((H, rows, CL), BF16),
        VM((H, rows, CL), BF16),
        VM((H, rows, CL), BF16),
        VM((H, rows, CL), BF16),
        VM((rows, CL), BF16),
        VM((e_rows, CE), BF16),
        VM((e_rows, CE), BF16),
        VM((CE, FE), BF16),
        VM((FE, CE), BF16),
        VM((e_rows, FE), BF16),
        VM((e_rows, FE), F32),
        VM((e_rows, CE), BF16),
        VM((2, CE, FE), F32),
        VM((2, CE // 2, FE), BF16),
        VM((2, CE // 2, FE), BF16),
        VM((CE // 2, FE), BF16),
        VM((CE // 2, FE), BF16),
        VM((CE // 2, FE), F32),
        VM((CE // 2, FE), BF16),
        VM((NZ, CE // 2 // NZ, FE), BF16),
        VM((2, 2, CE // 2, FE), BF16),
        pltpu.SemaphoreType.DMA((N_SEMS,)),
    ]
    anywhere = pl.BlockSpec(memory_space=pl.ANY)
    late_out, input_grad, grads = pl.pallas_call(
        functools.partial(kernel, (NS, NZ)),
        out_shape=(
            jax.ShapeDtypeStruct((rows, CL), BF16),
            jax.ShapeDtypeStruct((e_rows, CE), BF16),
            jax.ShapeDtypeStruct((2, 2, CE // 2, FE), BF16),
        ),
        in_specs=[anywhere] * 13,
        out_specs=(anywhere,) * 3,
        scratch_shapes=scratch,
        compiler_params=pltpu.CompilerParams(
            collective_id=0, has_side_effects=True, vmem_limit_bytes=60 * 1024 * 1024
        ),
        name="relay_step",
    )(
        late_sent[0],
        entry_rows,
        gain_first,
        shift_first,
        expand_late[0],
        gain_inner,
        shift_inner,
        reduce_late[0],
        early_saved[0],
        upstream_grad[0],
        exit_grad,
        expand_early[0],
        reduce_early[0],
    )
    grads = grads.reshape(2, CE, FE)
    return (
        late_out[None],
        input_grad[None],
        grads[0].astype(F32)[None],
        grads[1].T.astype(F32)[None],
    )


def solution(mesh):
    sections, devices = mesh.devices.shape
    split = Mesh(mesh.devices.reshape(sections, 2, devices // 4, 2), ("section", *DEV))
    return jax.shard_map(
        shards,
        mesh=split,
        in_specs=(
            P("section", DEV, None),
            P(DEV, None),
            P("section", None),
            P("section", None),
            P("section", None, DEV),
            P("section", DEV),
            P("section", DEV),
            P("section", DEV, None),
            P("section", DEV, None),
            P("section", DEV, None),
            P(DEV, None),
            P("section", None, None),
            P("section", None, None),
        ),
        out_specs=(
            P("section", DEV, None),
            P("section", DEV, None),
            P("section", None, None),
            P("section", None, None),
        ),
        check_vma=False,
    )
```

time: 299 us -> 120 us (0.40)
  the two profiles are of different devices: /device:TPU:12 before, /device:TPU:1 now
where the time goes in v1:
time: 120 us; the launch traced here: 118 us
  Pallas kernels  112 us (93%)
  local copies, waits for them, and re-layouts  4.16 us (3%)
  other arithmetic  1.26 us (1%)
    pallas_call x1, Pallas kernels, shards(): pl.pallas_call(functools.partial(kernel, (NS, NZ)), out_shape=(jax.ShapeD...  112 us

profile of v1, /device:TPU:1, one launch (start us, length us, event | category | flops | bytes accessed | tf_op | source)
XLA Modules:
  0.0 118.4 jit_solution(8216968306227989110)
XLA Ops:
  0.6 112.4 %relay_step.1 = (bf16[98,1024]{1,0:T(8,128)(2,1)}, bf16[1568,256]{1,0:T(8,128)(2,1)}, bf16[2,2,128,1024]{3,2,1,0:T(8,128)(2,1)}) custom-call(bf16[98,1024]{1,0:T(8,128)(2,1)} %bitcast.27, bf16[98,1024]{1,0:T(8,128)(2,1)} %entry_ref.1, f32[1,1024]{1,0:T(1,128)} %gain_first_ref.1, f32[1,1024]{1,0:T(1,128)} %shift_first_ref.1, bf16[1024,128]{1,0:T(8,128)(2,1)} %bitcast.24, ...), custom_call_target="tpu_custom_call" | custom-call | tf_op jit(solution)/shard_map/relay_step/pallas_call | solution.py:530
  113.0 1.3 %fusion = (bf16[1,2,128,1024]{3,2,1,0:T(8,128)(2,1)S(1)}, bf16[1,2,128,1024]{3,2,1,0:T(8,128)(2,1)S(1)}) fusion(bf16[2,2,128,1024]{3,2,1,0:T(8,128)(2,1)} %get-tuple-element.9), kind=kLoop, calls=%fused_computation.2 | loop fusion | bytes 2097152 | tf_op jit(solution)/shard_map/slice | solution.py:564
  114.3 0.1 bitcast_convert_fusion
  114.4 1.3 %copy.17 = f32[256,1024]{0,1:T(8,128)} copy(f32[256,1024]{1,0:T(8,128)S(1)} %bitcast_convert_fusion) | data formatting | bytes 2097152 | tf_op jit(solution)/shard_map/broadcast_in_dim | solution.py:564
  115.7 0.0 copy-start.1
  115.7 0.0 copy-start
  115.7 1.1 bitcast_convert_fusion.1
  116.9 0.0 copy-done.1
  116.9 0.7 copy.20
  117.5 0.0 copy-done
  117.5 0.9 copy.21
Async XLA Ops:
  115.7 1.1 copy-start.1
  115.7 1.8 %copy-start = (bf16[1568,256]{1,0:T(8,128)(2,1)S(1)}, bf16[1568,256]{1,0:T(8,128)(2,1)}, u32[]{:S(2)}) copy-start(bf16[1568,256]{1,0:T(8,128)(2,1)} %get-tuple-element.8) | copy-start | bytes 2408452

commit v2 on v1

v2 whole, which is shorter than its diff:
```python
import functools
import math

import jax
import jax.numpy as jnp
from jax import lax
from jax.experimental import pallas as pl
from jax.experimental.pallas import tpu as pltpu
from jax.sharding import Mesh
from jax.sharding import PartitionSpec as P

DEV = ("b", "z", "c")
MESH = pl.DeviceIdType.MESH
F32 = jnp.float32
BF16 = jnp.bfloat16
EPS = 1e-05
Q = 4
PIECES = 7
BLOCK = 256
N_SEMS = 400
W2_AT = 2
EARLY_FIRST = 3
HELD = 4
PLAN = "mmmmmmmmm" + "msmmsms" + "msmssssmssm" + "mmmsm" + "msmmm"
FAR_FIRST = (4, 3, 5, 2, 6, 1, 7, 0)


def silu(v):
    return v * jax.nn.sigmoid(v)


def affine(sums, squares, count, gain, shift):
    average = sums / count
    second = squares / count
    spread = gain * lax.rsqrt(second - average * average + EPS)
    return spread, shift - average * spread


def kernel(
    sizes,
    late_ref,
    entry_ref,
    gain_first_ref,
    shift_first_ref,
    expand_late_ref,
    gain_inner_ref,
    shift_inner_ref,
    reduce_late_ref,
    saved_ref,
    up_ref,
    exit_ref,
    expand_early_ref,
    reduce_early_ref,
    LO,
    OG,
    GE,
    OR,
    S,
    ZST,
    ZT,
    FST,
    GS,
    G,
    F,
    W1,
    W2,
    GI,
    SI,
    IST,
    INN,
    PT,
    SC,
    SA,
    RC,
    RA,
    SV,
    GR,
    WE1,
    WE2,
    ACT,
    DS,
    ACC,
    SD,
    RD,
    SX,
    RX,
    TF,
    SZ,
    RZ,
    FIN,
    sems,
):
    NS, NZ = sizes
    H = NZ // 2
    rows, CL = S.shape
    CQ = CL // Q
    HID = expand_late_ref.shape[1]
    e_rows, CE = SV.shape
    FE = WE1.shape[1]
    PR = e_rows // PIECES
    ZR = CE // 2 // NZ
    late_count = rows * NZ * 4

    s = lax.axis_index("section")
    b = lax.axis_index("b")
    z = lax.axis_index("z")
    c = lax.axis_index("c")
    ahead = lax.rem(s + 1, NS)
    behind = lax.rem(s + NS - 1, NS)
    other_b = 1 - b
    other_c = 1 - c

    def zat(d):
        return lax.rem(z + d + NZ, NZ)

    def group(k):
        where = {}
        if k & 2:
            where["b"] = other_b
        if k & 1:
            where["c"] = other_c
        return where

    used = [0]
    sent = []

    def new_sem():
        used[0] += 1
        return sems.at[used[0] - 1]

    def remote(src, dst, to, pair=None):
        pair = pair or (new_sem(), new_sem())
        return pltpu.make_async_remote_copy(
            src_ref=src, dst_ref=dst, send_sem=pair[0], recv_sem=pair[1], device_id=to, device_id_type=MESH
        )

    def send(src, dst, to):
        copy = remote(src, dst, to)
        copy.start()
        sent.append(copy)
        return copy

    def load(src, dst):
        copy = pltpu.make_async_copy(src, dst, new_sem())
        copy.start()
        return copy

    def cols(q):
        return slice(q * CQ, (q + 1) * CQ)

    barrier = pltpu.get_barrier_semaphore()
    greeted = [{"z": zat(d)} for d in range(1, NZ)] + [group(k) for k in (1, 2, 3)]
    greeted += [{"section": ahead, **group(k)} for k in range(4)]
    greeted += [{"section": behind, **group(k)} for k in range(4)]
    with jax.named_scope("greet"):
        for to in greeted:
            pl.semaphore_signal(barrier, inc=1, device_id=to, device_id_type=MESH)

    last = s == NS - 1
    sem_s = new_sem()
    take_late = pltpu.make_async_copy(late_ref, S, sem_s)
    take_entry = pltpu.make_async_copy(entry_ref, S, sem_s)

    @pl.when(last)
    def _():
        take_entry.start()

    @pl.when(jnp.logical_not(last))
    def _():
        take_late.start()

    load_saved = load(saved_ref, SV)
    load_we1 = load(expand_early_ref, WE1)
    load_we2 = load(reduce_early_ref, WE2)
    load_gf = load(gain_first_ref, GS.at[0])
    load_sf = load(shift_first_ref, GS.at[1])
    load_w1 = load(expand_late_ref, W1.at[:, 0:HID])
    load_w2 = load(reduce_late_ref, W2.at[0:HID, :])
    load_gi = load(gain_inner_ref, GI.at[0])
    load_si = load(shift_inner_ref, SI.at[0])

    with jax.named_scope("own_stats"):
        take_late.wait()
        for q in range(Q):
            values = S[:, cols(q)].astype(F32)
            ZST[0, 0:1, cols(q)] = jnp.sum(values, axis=0, keepdims=True)
            ZST[0, 1:2, cols(q)] = jnp.sum(values * values, axis=0, keepdims=True)

    with jax.named_scope("barrier"):
        pl.semaphore_wait(barrier, len(greeted))

    with jax.named_scope("sends"):
        shift_late = [send(S.at[:, cols(q)], G.at[0, :, cols(q)], {"section": ahead}) for q in range(Q)]
        z_stats = [send(ZST.at[0], ZST.at[d], {"z": zat(d)}) for d in range(1, NZ)]

        w1_near = send(expand_late_ref, W1.at[:, HID : 2 * HID], group(1))
        w2_near = send(reduce_late_ref, W2.at[HID : 2 * HID, :], group(1))
        gains = []
        for k in (1, 2, 3):
            gains.append(send(gain_inner_ref, GI.at[k], group(k)))
            gains.append(send(shift_inner_ref, SI.at[k], group(k)))

    first_grad = s == 0
    shift_grad = []
    for p in range(PIECES):
        piece = slice(p * PR, (p + 1) * PR)
        pair = (new_sem(), new_sem())
        one = remote(exit_ref.at[piece], GR.at[piece], {"section": behind}, pair)
        two = remote(up_ref.at[piece], GR.at[piece], {"section": behind}, pair)
        shift_grad.append((one, two))

    def start_grad(p):
        one, two = shift_grad[p]
        pl.when(first_grad)(one.start)
        pl.when(jnp.logical_not(first_grad))(two.start)
        sent.append(two)

    w1_far = remote(expand_late_ref, W1.at[:, 2 * HID : 3 * HID], group(2))
    w2_far = remote(reduce_late_ref, W2.at[2 * HID : 3 * HID, :], group(2))

    def start_far(copy):
        copy.start()
        sent.append(copy)

    bulk = [functools.partial(start_grad, p) for p in range(PIECES)]
    bulk.insert(W2_AT, functools.partial(start_far, w2_far))

    def tick(n=1, keep=0):
        for _ in range(n):
            if len(bulk) > keep:
                bulk.pop(0)()

    with jax.named_scope("load_wait"):
        load_saved.wait()
        load_we1.wait()
        load_we2.wait()

    def early_rows(p):
        return pl.ds(pl.multiple_of(p * PR, PR), PR)

    def early_one(p, carry):
        at = early_rows(p)
        saved = SV[at, :]
        for f in range(0, FE, BLOCK):
            pre = jnp.dot(saved, WE1[:, f : f + BLOCK], preferred_element_type=F32)
            sigma = jax.nn.sigmoid(pre)
            ACT[at, f : f + BLOCK] = (pre * sigma).astype(BF16)
            DS[at, f : f + BLOCK] = sigma * (1.0 + pre * (1.0 - sigma))
        return carry

    with jax.named_scope("early_one"):
        lax.fori_loop(0, PIECES, early_one, 0)

        ACC[...] = jnp.zeros(ACC.shape, F32)

    def early_two(p):
        at = slice(p * PR, (p + 1) * PR)
        with jax.named_scope("grad_wait"):
            shift_grad[p][1].wait_recv()
        with jax.named_scope("early_two"):
            grad = GR[at, :]
            saved = SV[at, :]
            result = grad.astype(F32)
            for f in range(0, FE, BLOCK):
                block = slice(f, f + BLOCK)
                back = lax.dot_general(grad, WE2[block, :], (((1,), (1,)), ((), ())), preferred_element_type=F32)
                slope = (back * DS[at, block]).astype(BF16)
                ACC[0, :, block] += lax.dot_general(saved, slope, (((0,), (0,)), ((), ())), preferred_element_type=F32)
                ACC[1, :, block] += lax.dot_general(
                    ACT[at, block], grad, (((0,), (0,)), ((), ())), preferred_element_type=F32
                )
                result += lax.dot_general(slope, WE1[:, block], (((1,), (1,)), ((), ())), preferred_element_type=F32)
            OG[at, :] = result.astype(BF16)

    hops_c, hops_a = [], []

    def forward(t, q):
        if t < H or q < Q // 2:
            hops_c.append((t, q, send(G.at[t - 1, :, cols(q)], G.at[t, :, cols(q)], {"z": zat(1)})))
        if t < H or q >= Q // 2:
            src, dst = (NZ - t + 1) % NZ, NZ - t
            hops_a.append((t, q, send(G.at[src, :, cols(q)], G.at[dst, :, cols(q)], {"z": zat(-1)})))

    def arrived(t, q):
        for hops in (hops_c, hops_a):
            for u, r, copy in hops:
                if (u, r) == (t, q):
                    copy.wait_recv()

    with jax.named_scope("zstats_wait"):
        for copy in z_stats:
            copy.wait_recv()
    total = ZST[0]
    for d in range(1, NZ):
        total = total + ZST[d]
    ZT[...] = total
    first_stats = [send(ZT, FST.at[k], {"section": ahead, **group(k)}) for k in range(4)]
    start_far(w1_far)
    tick()
    for q in range(Q):
        with jax.named_scope("shift_wait"):
            shift_late[q].wait_recv()
        forward(1, q)

    if H > 1:
        with jax.named_scope("hop1"):
            for q in range(Q):
                arrived(1, q)
                forward(2, q)
                if q % 2:
                    tick(keep=HELD)

    with jax.named_scope("fstats_wait"):
        for copy in first_stats:
            copy.wait_recv()
    load_gf.wait()
    load_sf.wait()
    sums = FST[0] + FST[1] + FST[2] + FST[3]
    spread, offset = affine(sums[0:1], sums[1:2], late_count, GS[0], GS[1])

    def first_of(slot):
        for q in range(Q):
            at = cols(q)
            values = G[slot, :, at].astype(F32) * spread[:, at] + offset[:, at]
            F[slot, :, at] = silu(values).astype(BF16)

    stats = [0.0, 0.0]

    def inner_of(slot):
        inner = jnp.dot(F[slot], W1[...], preferred_element_type=F32)
        INN[slot] = inner
        stats[0] += jnp.sum(inner, axis=0, keepdims=True)
        stats[1] += jnp.sum(inner * inner, axis=0, keepdims=True)

    def forward_w1():
        with jax.named_scope("w1_wait"):
            w1_far.wait_recv()
        return send(W1.at[:, 2 * HID : 3 * HID], W1.at[:, 3 * HID :], group(1))

    with jax.named_scope("first0"):
        first_of(0)
    done = []
    for t in range(2, H):
        with jax.named_scope(f"hop{t}"):
            for q in range(Q):
                arrived(t, q)
                forward(t + 1, q)
                if q % 2:
                    tick(keep=HELD)
        if t == 2:
            w1_fwd = forward_w1()
        for slot in (t - 1, NZ - t + 1):
            with jax.named_scope("first"):
                first_of(slot)
            done.append(slot)

    if H <= 2:
        w1_fwd = forward_w1()
    with jax.named_scope("w1_fwd_wait"):
        load_w1.wait()
        w1_near.wait_recv()
        w1_fwd.wait_recv()
    with jax.named_scope("inner5"):
        for slot in [0] + done:
            inner_of(slot)
    for slot in (H - 1, H + 1):
        if slot not in done and slot != 0 and H > 1:
            with jax.named_scope("first_inner"):
                first_of(slot)
                inner_of(slot)
    with jax.named_scope("hopH"):
        for q in range(Q):
            arrived(H, q)
    with jax.named_scope("first_inner"):
        first_of(H)
        inner_of(H)

    order = [d for d in FAR_FIRST if d < NZ]
    cuts = [(0, NZ // 2), (NZ // 2, NZ)]
    factor = 1.0 / math.sqrt(e_rows * NZ * 4)

    def acc_rows(half, d):
        return pl.ds(pl.multiple_of(half * (CE // 2) + zat(d) * ZR, ZR), ZR)

    pair_sums, x_sums, z_sums, z_back, x_back, c_back, c_back_two = {}, {}, {}, {}, {}, {}, {}

    def pair_send(h, k):
        lo, hi = cuts[k]
        for i in range(lo, hi):
            SD[h, i] = ACC[other_c, acc_rows(other_b if h == 0 else b, order[i]), :].astype(BF16)
        pair_sums[h, k] = send(SD.at[h, lo:hi], RD.at[h, lo:hi], group(1))

    def x_send(k):
        lo, hi = cuts[k]
        pair_sums[0, k].wait_recv()
        for i in range(lo, hi):
            SX[i] = (ACC[c, acc_rows(other_b, order[i]), :] + RD[0, i].astype(F32)).astype(BF16)
        x_sums[k] = send(SX.at[lo:hi], RX.at[lo:hi], group(2))

    def z_send(k):
        lo, hi = cuts[k]
        pair_sums[1, k].wait_recv()
        x_sums[k].wait_recv()
        for i in range(lo, hi):
            d = order[i]
            value = ACC[c, acc_rows(b, d), :] + RD[1, i].astype(F32) + RX[i].astype(F32)
            if d == 0:
                TF[...] = value
            else:
                SZ[d] = value.astype(BF16)
                z_sums[d] = send(SZ.at[d], RZ.at[d], {"z": zat(d)})

    def fin(core, half, d):
        return FIN.at[core, half, pl.ds(pl.multiple_of(zat(d) * ZR, ZR), ZR)]

    def back_to_x_and_core(d):
        piece = fin(c, b, d)
        x_back[d] = send(piece, piece, group(2))
        c_back[d] = send(piece, piece, group(1))

    def back_across(d):
        x_back[d].wait_recv()
        piece = fin(c, other_b, d)
        c_back_two[d] = send(piece, piece, group(1))

    def z_finish():
        value = TF[...]
        for d in order[::-1]:
            if d:
                z_sums[d].wait_recv()
                value = value + RZ[d].astype(F32)
        FIN[c, b, pl.ds(pl.multiple_of(z * ZR, ZR), ZR), :] = (value * factor).astype(BF16)
        own = fin(c, b, 0)
        for d in order[::-1]:
            if d:
                z_back[d] = send(own, own, {"z": zat(d)})
        back_to_x_and_core(0)

    def z_forward(d):
        z_back[d].wait_recv()
        back_to_x_and_core(-d)

    IST[0, 0:1] = stats[0]
    IST[0, 1:2] = stats[1]
    inner_stats = [send(IST.at[0], IST.at[k], group(k)) for k in (1, 2, 3)]

    tick(len(bulk))
    for p in range(EARLY_FIRST):
        early_two(p)

    with jax.named_scope("w2_wait"):
        w2_far.wait_recv()
    w2_fwd = send(W2.at[2 * HID : 3 * HID, :], W2.at[3 * HID :, :], group(1))
    with jax.named_scope("istats_wait"):
        load_w2.wait()
        load_gi.wait()
        load_si.wait()
        w2_near.wait_recv()
        for copy in gains:
            copy.wait_recv()
        for copy in inner_stats:
            copy.wait_recv()
    spreads, offsets = [], []
    for k in range(4):
        piece = IST[0, :, k * HID : (k + 1) * HID]
        for d in (1, 2, 3):
            j = k ^ d
            piece = piece + IST[d, :, j * HID : (j + 1) * HID]
        one, two = affine(piece[0:1], piece[1:2], late_count, GI[k], SI[k])
        spreads.append(one)
        offsets.append(two)
    spread_two = jnp.concatenate(spreads, axis=1)
    offset_two = jnp.concatenate(offsets, axis=1)
    with jax.named_scope("w2_fwd_wait"):
        w2_fwd.wait_recv()

    def partial_of(slot):
        hidden = silu(INN[slot] * spread_two + offset_two).astype(BF16)
        PT[slot] = jnp.dot(hidden, W2[...], preferred_element_type=F32)

    sums_c, sums_a = {}, {}

    def sum_hop(t, q):
        at = cols(q)
        for slot, sums_d, S_, R_, step, half in (
            (NZ - (H - t), sums_c, SC, RC, 1, q < Q // 2),
            (H - t, sums_a, SA, RA, -1, q >= Q // 2),
        ):
            if t == 0 and not half:
                continue
            value = PT[slot, :, at]
            if t > 1 or (t == 1 and half):
                sums_d[t - 1, q].wait_recv()
                value = value + R_[t - 1, :, at].astype(F32)
            S_[t, :, at] = value.astype(BF16)
            sums_d[t, q] = send(S_.at[t, :, at], R_.at[t, :, at], {"z": zat(step)})

    def late_final(q):
        at = cols(q)
        value = PT[0, :, at]
        if H > 1 or q < Q // 2:
            sums_c[H - 1, q].wait_recv()
            value = value + RC[H - 1, :, at].astype(F32)
        if H > 1 or q >= Q // 2:
            sums_a[H - 1, q].wait_recv()
            value = value + RA[H - 1, :, at].astype(F32)
        LO[:, at] = (G[0, :, at].astype(F32) + value).astype(BF16)

    def partials(t):
        if t == 0:
            partial_of(H)
        elif t == H:
            partial_of(0)
        else:
            partial_of(NZ - (H - t))
            partial_of(H - t)

    near_first = [d for d in order[::-1] if d]
    side = [("early_two", functools.partial(early_two, p)) for p in range(EARLY_FIRST, PIECES)]
    side += [("pair_send", functools.partial(pair_send, h, k)) for h in (0, 1) for k in (0, 1)]
    side += [("x_send", functools.partial(x_send, k)) for k in (0, 1)]
    side += [("z_send", functools.partial(z_send, k)) for k in (0, 1)]
    side.append(("z_finish", z_finish))
    side += [("z_forward", functools.partial(z_forward, d)) for d in near_first[:2]]
    side.append(("across", functools.partial(back_across, 0)))
    for at, d in enumerate(near_first[2:]):
        side.append(("z_forward", functools.partial(z_forward, d)))
        if at:
            side.append(("across", functools.partial(back_across, -near_first[at - 1])))
    main = [("partials", functools.partial(partials, 0))]
    main += [("sum0", functools.partial(sum_hop, 0, q)) for q in range(Q)]
    main += [("partials", functools.partial(partials, t)) for t in range(1, H + 1)]
    main += [(f"sum{t}", functools.partial(sum_hop, t, q)) for t in range(1, H) for q in range(Q)]
    main += [("late_final", functools.partial(late_final, q)) for q in range(Q)]
    for step in PLAN:
        which = main if step == "m" else side
        if which:
            name, go = which.pop(0)
            with jax.named_scope(name):
                go()
    for name, go in main + side:
        with jax.named_scope(name):
            go()

    with jax.named_scope("across"):
        for d in near_first:
            if -d not in c_back_two:
                back_across(-d)
    with jax.named_scope("c_back"):
        for d in [0] + [-d for d in near_first]:
            c_back[d].wait_recv()
            c_back_two[d].wait_recv()
    with jax.named_scope("outputs"):
        for half in (0, 1):
            at = slice(half * (CE // 2), (half + 1) * (CE // 2))
            GE[at, :] = FIN[0, half].astype(F32)
            for f in range(0, FE, BLOCK):
                OR[f + half * (CE // 2) : f + (half + 1) * (CE // 2), :] = FIN[1, half, :, f : f + BLOCK].astype(F32)

    with jax.named_scope("drain"):
        for copy in sent:
            copy.wait_send()


def place(*refs):
    sems = refs[8]
    copies = [pltpu.make_async_copy(refs[i], refs[4 + i], sems.at[i]) for i in range(4)]
    for copy in copies:
        copy.start()
    for copy in copies:
        copy.wait()


def shards(
    late_sent,
    entry_rows,
    gain_first,
    shift_first,
    expand_late,
    gain_inner,
    shift_inner,
    reduce_late,
    early_saved,
    upstream_grad,
    exit_grad,
    expand_early,
    reduce_early,
):
    rows, CL = entry_rows.shape
    e_rows, CE = exit_grad.shape
    FE = expand_early.shape[2]
    HID = expand_late.shape[2]
    NS, NZ = lax.axis_size("section"), lax.axis_size("z")
    H = NZ // 2
    VM = pltpu.VMEM
    scratch = [
        VM((rows, CL), BF16),
        VM((NZ, 2, CL), F32),
        VM((2, CL), F32),
        VM((4, 2, CL), F32),
        VM((2, 1, CL), F32),
        VM((NZ, rows, CL), BF16),
        VM((NZ, rows, CL), BF16),
        VM((CL, 4 * HID), BF16),
        VM((4 * HID, CL), BF16),
        VM((4, 1, HID), F32),
        VM((4, 1, HID), F32),
        VM((4, 2, 4 * HID), F32),
        VM((NZ, rows, 4 * HID), F32),
        VM((NZ, rows, CL), F32),
        VM((H, rows, CL), BF16),
        VM((H, rows, CL), BF16),
        VM((H, rows, CL), BF16),
        VM((H, rows, CL), BF16),
        VM((e_rows, CE), BF16),
        VM((e_rows, CE), BF16),
        VM((CE, FE), BF16),
        VM((FE, CE), BF16),
        VM((e_rows, FE), BF16),
        VM((e_rows, FE), F32),
        VM((2, CE, FE), F32),
        VM((2, NZ, CE // 2 // NZ, FE), BF16),
        VM((2, NZ, CE // 2 // NZ, FE), BF16),
        VM((NZ, CE // 2 // NZ, FE), BF16),
        VM((NZ, CE // 2 // NZ, FE), BF16),
        VM((CE // 2 // NZ, FE), F32),
        VM((NZ, CE // 2 // NZ, FE), BF16),
        VM((NZ, CE // 2 // NZ, FE), BF16),
        VM((2, 2, CE // 2, FE), BF16),
        pltpu.SemaphoreType.DMA((N_SEMS,)),
    ]
    hbm = pl.BlockSpec(memory_space=pltpu.HBM)
    vmem = pl.BlockSpec(memory_space=pltpu.VMEM)
    late_out, input_grad, grad_expand, grad_reduce = pl.pallas_call(
        functools.partial(kernel, (NS, NZ)),
        out_shape=(
            VM((rows, CL), BF16),
            VM((e_rows, CE), BF16),
            VM((CE, FE), F32),
            VM((FE, CE), F32),
        ),
        in_specs=[hbm] * 13,
        out_specs=(vmem,) * 4,
        scratch_shapes=scratch,
        compiler_params=pltpu.CompilerParams(
            collective_id=0, has_side_effects=True, vmem_limit_bytes=44 * 1024 * 1024
        ),
        name="relay_step",
    )(
        *(
            pltpu.with_memory_space_constraint(x, pltpu.HBM)
            for x in (
                late_sent[0],
                entry_rows,
                gain_first,
                shift_first,
                expand_late[0],
                gain_inner,
                shift_inner,
                reduce_late[0],
                early_saved[0],
                upstream_grad[0],
                exit_grad,
                expand_early[0],
                reduce_early[0],
            )
        )
    )
    results = (late_out, input_grad, grad_expand, grad_reduce)
    results = pl.pallas_call(
        place,
        out_shape=tuple(jax.ShapeDtypeStruct(x.shape, x.dtype) for x in results),
        in_specs=[vmem] * 4,
        out_specs=(pl.BlockSpec(memory_space=pl.ANY),) * 4,
        scratch_shapes=[pltpu.SemaphoreType.DMA((4,))],
        compiler_params=pltpu.CompilerParams(vmem_limit_bytes=4 * 1024 * 1024),
        name="place",
    )(*results)
    return tuple(x[None] for x in results)


def solution(mesh):
    sections, devices = mesh.devices.shape
    split = Mesh(mesh.devices.reshape(sections, 2, devices // 4, 2), ("section", *DEV))
    return jax.shard_map(
        shards,
        mesh=split,
        in_specs=(
            P("section", DEV, None),
            P(DEV, None),
            P("section", None),
            P("section", None),
            P("section", None, DEV),
            P("section", DEV),
            P("section", DEV),
            P("section", DEV, None),
            P("section", DEV, None),
            P("section", DEV, None),
            P(DEV, None),
            P("section", None, None),
            P("section", None, None),
        ),
        out_specs=(
            P("section", DEV, None),
            P("section", DEV, None),
            P("section", None, None),
            P("section", None, None),
        ),
        check_vma=False,
    )
```

time: 120 us -> 86.4 us (0.72); the launches traced: 118 us -> 86.3 us
  Pallas kernels: 112 us -> 85.6 us
  local copies, waits for them, and re-layouts: 4.16 us -> 0 us
  other arithmetic: 1.26 us -> 0 us
    pallas_call x1 -> x2, Pallas kernels: 112 us -> 85.6 us  [the longest x1 83.9 us: shards(): pl.pallas_call(functools.partial(kernel, (NS, NZ)), out_shape=(VM((rows,...]
    unnamed x6 -> x0, local copies, waits for them, and re-layouts: 1.57 us -> none
    broadcast_in_dim x1 -> x0, local copies, waits for them, and re-layouts: 1.31 us -> none  [shards(): grads[1].T.astype(F32)[None]]
    slice x1 -> x0, local copies, waits for them, and re-layouts: 1.27 us -> none  [shards(): grads[1].T.astype(F32)[None]]
where the time goes in v2:
time: 86.4 us; the launch traced here: 86.3 us
  Pallas kernels  85.6 us (99%)
    pallas_call x1, Pallas kernels, shards(): pl.pallas_call(functools.partial(kernel, (NS, NZ)), out_shape=(VM((rows,...  83.9 us

profile of v2, /device:TPU:1, one launch (start us, length us, event | category | flops | bytes accessed | tf_op | source)
XLA Modules:
  0.0 86.3 jit_solution(13425460807813097428)
XLA Ops:
  0.6 83.9 %relay_step.1 = (bf16[98,1024]{1,0:T(8,128)(2,1)S(1)}, bf16[1568,256]{1,0:T(8,128)(2,1)S(1)}, f32[256,1024]{1,0:T(8,128)S(1)}, f32[1024,256]{1,0:T(8,128)S(1)}) custom-call(bf16[98,1024]{1,0:T(8,128)(2,1)} %bitcast.17, bf16[98,1024]{1,0:T(8,128)(2,1)} %entry_ref.1, f32[1,1024]{1,0:T(1,128)} %gain_first_ref.1, f32[1,1024]{1,0:T(1,128)} %shift_first_ref.1, ...), custom_call_target="tpu_custom_call" | custom-call | tf_op jit(solution)/shard_map/relay_step/pallas_call | solution.py:634
  84.6 1.7 %place.1 = (bf16[98,1024]{1,0:T(8,128)(2,1)}, bf16[1568,256]{1,0:T(8,128)(2,1)}, f32[256,1024]{1,0:T(8,128)}, f32[1024,256]{1,0:T(8,128)}) custom-call(bf16[98,1024]{1,0:T(8,128)(2,1)S(1)} %get-tuple-element.12.refs_0_, bf16[1568,256]{1,0:T(8,128)(2,1)S(1)} %get-tuple-element.13.refs_1_, f32[256,1024]{1,0:T(8,128)S(1)} %get-tuple-element.14.refs_2_, ...), custom_call_target="tpu_custom_call" | custom-call | tf_op jit(solution)/shard_map/place/pallas_call | solution.py:670

commit v3 on v2

--- a/solution.py
+++ b/solution.py
@@ -18,10 +18,17 @@
 PIECES = 7
 BLOCK = 256
 N_SEMS = 400
-W2_AT = 2
-EARLY_FIRST = 3
-HELD = 4
-PLAN = "mmmmmmmmm" + "msmmsms" + "msmssssmssm" + "mmmsm" + "msmmm"
+PLAN = (
+    "Z0 Z1 I W0",
+    "B0 ZF W1 B1",
+    "12 13 R1 A0",
+    "20 21 22 R2",
+    "A7 A1 23 30",
+    "31 R3 A6 A2",
+    "32 33 R4 A5",
+    "A3 0f 1f 2f",
+    "3f A4",
+)
 FAR_FIRST = (4, 3, 5, 2, 6, 1, 7, 0)
 
 
@@ -68,6 +75,7 @@
     SI,
     IST,
     INN,
+    HB,
     PT,
     SC,
     SA,
@@ -216,19 +224,23 @@
         sent.append(two)
 
     w1_far = remote(expand_late_ref, W1.at[:, 2 * HID : 3 * HID], group(2))
-    w2_far = remote(reduce_late_ref, W2.at[2 * HID : 3 * HID, :], group(2))
+    half_cols = (slice(0, CL // 2), slice(CL // 2, CL))
+    w2_far = [
+        remote(reduce_late_ref.at[:, at], W2.at[2 * HID : 3 * HID, at], group(2)) for at in half_cols
+    ]
 
     def start_far(copy):
         copy.start()
         sent.append(copy)
 
-    bulk = [functools.partial(start_grad, p) for p in range(PIECES)]
-    bulk.insert(W2_AT, functools.partial(start_far, w2_far))
-
-    def tick(n=1, keep=0):
+    bulk = [functools.partial(start_grad, p) for p in range(PIECES)] + [functools.partial(start_far, w1_far)]
+
+    def tick(n=1):
         for _ in range(n):
-            if len(bulk) > keep:
+            if bulk:
                 bulk.pop(0)()
+
+    tick()
 
     with jax.named_scope("load_wait"):
         load_saved.wait()
@@ -249,7 +261,7 @@
         return carry
 
     with jax.named_scope("early_one"):
-        lax.fori_loop(0, PIECES, early_one, 0)
+        lax.fori_loop(0, PIECES - 2, early_one, 0)
 
         ACC[...] = jnp.zeros(ACC.shape, F32)
 
@@ -287,6 +299,14 @@
                 if (u, r) == (t, q):
                     copy.wait_recv()
 
+    def shift_forward(q):
+        with jax.named_scope("shift_wait"):
+            shift_late[q].wait_recv()
+        forward(1, q)
+
+    shift_forward(0)
+    lax.fori_loop(PIECES - 2, PIECES, early_one, 0)
+    shift_forward(1)
     with jax.named_scope("zstats_wait"):
         for copy in z_stats:
             copy.wait_recv()
@@ -295,12 +315,9 @@
         total = total + ZST[d]
     ZT[...] = total
     first_stats = [send(ZT, FST.at[k], {"section": ahead, **group(k)}) for k in range(4)]
-    start_far(w1_far)
-    tick()
-    for q in range(Q):
-        with jax.named_scope("shift_wait"):
-            shift_late[q].wait_recv()
-        forward(1, q)
+    tick(2)
+    for q in range(2, Q):
+        shift_forward(q)
 
     if H > 1:
         with jax.named_scope("hop1"):
@@ -308,7 +325,7 @@
                 arrived(1, q)
                 forward(2, q)
                 if q % 2:
-                    tick(keep=HELD)
+                    tick()
 
     with jax.named_scope("fstats_wait"):
         for copy in first_stats:
@@ -332,49 +349,6 @@
         stats[0] += jnp.sum(inner, axis=0, keepdims=True)
         stats[1] += jnp.sum(inner * inner, axis=0, keepdims=True)
 
-    def forward_w1():
-        with jax.named_scope("w1_wait"):
-            w1_far.wait_recv()
-        return send(W1.at[:, 2 * HID : 3 * HID], W1.at[:, 3 * HID :], group(1))
-
-    with jax.named_scope("first0"):
-        first_of(0)
-    done = []
-    for t in range(2, H):
-        with jax.named_scope(f"hop{t}"):
-            for q in range(Q):
-                arrived(t, q)
-                forward(t + 1, q)
-                if q % 2:
-                    tick(keep=HELD)
-        if t == 2:
-            w1_fwd = forward_w1()
-        for slot in (t - 1, NZ - t + 1):
-            with jax.named_scope("first"):
-                first_of(slot)
-            done.append(slot)
-
-    if H <= 2:
-        w1_fwd = forward_w1()
-    with jax.named_scope("w1_fwd_wait"):
-        load_w1.wait()
-        w1_near.wait_recv()
-        w1_fwd.wait_recv()
-    with jax.named_scope("inner5"):
-        for slot in [0] + done:
-            inner_of(slot)
-    for slot in (H - 1, H + 1):
-        if slot not in done and slot != 0 and H > 1:
-            with jax.named_scope("first_inner"):
-                first_of(slot)
-                inner_of(slot)
-    with jax.named_scope("hopH"):
-        for q in range(Q):
-            arrived(H, q)
-    with jax.named_scope("first_inner"):
-        first_of(H)
-        inner_of(H)
-
     order = [d for d in FAR_FIRST if d < NZ]
     cuts = [(0, NZ // 2), (NZ // 2, NZ)]
     factor = 1.0 / math.sqrt(e_rows * NZ * 4)
@@ -382,7 +356,9 @@
     def acc_rows(half, d):
         return pl.ds(pl.multiple_of(half * (CE // 2) + zat(d) * ZR, ZR), ZR)
 
-    pair_sums, x_sums, z_sums, z_back, x_back, c_back, c_back_two = {}, {}, {}, {}, {}, {}, {}
+    pair_sums, x_sums, z_sums, x_back, c_back, c_back_two = {}, {}, {}, {}, {}, {}
+    back_c, back_a = {}, {}
+    HALF = FE // 2
 
     def pair_send(h, k):
         lo, hi = cuts[k]
@@ -430,28 +406,84 @@
                 z_sums[d].wait_recv()
                 value = value + RZ[d].astype(F32)
         FIN[c, b, pl.ds(pl.multiple_of(z * ZR, ZR), ZR), :] = (value * factor).astype(BF16)
-        own = fin(c, b, 0)
-        for d in order[::-1]:
-            if d:
-                z_back[d] = send(own, own, {"z": zat(d)})
+        z_back(1)
         back_to_x_and_core(0)
 
-    def z_forward(d):
-        z_back[d].wait_recv()
-        back_to_x_and_core(-d)
+    def z_back(t):
+        for back, step in ((back_c, 1), (back_a, -1)):
+            piece = fin(c, b, -step * (t - 1))
+            if t == H:
+                piece = piece.at[:, 0:HALF] if step == 1 else piece.at[:, HALF:FE]
+            back[t] = send(piece, piece, {"z": zat(step)})
+
+    def z_forward(t):
+        back_c[t].wait_recv()
+        back_a[t].wait_recv()
+        if t < H:
+            z_back(t + 1)
+            back_to_x_and_core(-t)
+            back_to_x_and_core(t)
+        else:
+            back_to_x_and_core(H)
+
+    def both(*slots):
+        for slot in slots:
+            with jax.named_scope("first"):
+                first_of(slot)
+
+    both(0)
+    early_two(0)
+    early = 1
+    for t in range(2, H):
+        with jax.named_scope(f"hop{t}"):
+            for q in range(Q):
+                arrived(t, q)
+                forward(t + 1, q)
+                if q % 2:
+                    tick()
+        both(t - 1, NZ - t + 1)
+        early_two(early)
+        early_two(early + 1)
+        early += 2
+    tick(len(bulk))
+    with jax.named_scope("hopH"):
+        for q in range(Q):
+            arrived(H, q)
+    both(H - 1, H + 1, H)
+    for p in range(early, PIECES):
+        early_two(p)
+    for h in (0, 1):
+        for k in (0, 1):
+            pair_send(h, k)
+    with jax.named_scope("X0"):
+        x_send(0)
+    with jax.named_scope("X1"):
+        x_send(1)
+    with jax.named_scope("w1_wait"):
+        w1_far.wait_recv()
+    w1_fwd = send(W1.at[:, 2 * HID : 3 * HID], W1.at[:, 3 * HID :], group(1))
+    with jax.named_scope("w1_fwd_wait"):
+        load_w1.wait()
+        w1_near.wait_recv()
+        w1_fwd.wait_recv()
+    with jax.named_scope("inner"):
+        for slot in range(NZ):
+            inner_of(slot)
 
     IST[0, 0:1] = stats[0]
     IST[0, 1:2] = stats[1]
     inner_stats = [send(IST.at[0], IST.at[k], group(k)) for k in (1, 2, 3)]
 
-    tick(len(bulk))
-    for p in range(EARLY_FIRST):
-        early_two(p)
-
-    with jax.named_scope("w2_wait"):
-        w2_far.wait_recv()
-    w2_fwd = send(W2.at[2 * HID : 3 * HID, :], W2.at[3 * HID :, :], group(1))
-    with jax.named_scope("istats_wait"):
+    start_far(w2_far[0])
+    start_far(w2_far[1])
+
+    late = {}
+
+    def second_weight(h):
+        w2_far[h].wait_recv()
+        late["fwd", h] = send(W2.at[2 * HID : 3 * HID, half_cols[h]], W2.at[3 * HID :, half_cols[h]], group(1))
+
+    def second_norm():
         load_w2.wait()
         load_gi.wait()
         load_si.wait()
@@ -460,40 +492,53 @@
             copy.wait_recv()
         for copy in inner_stats:
             copy.wait_recv()
-    spreads, offsets = [], []
-    for k in range(4):
-        piece = IST[0, :, k * HID : (k + 1) * HID]
-        for d in (1, 2, 3):
-            j = k ^ d
-            piece = piece + IST[d, :, j * HID : (j + 1) * HID]
-        one, two = affine(piece[0:1], piece[1:2], late_count, GI[k], SI[k])
-        spreads.append(one)
-        offsets.append(two)
-    spread_two = jnp.concatenate(spreads, axis=1)
-    offset_two = jnp.concatenate(offsets, axis=1)
-    with jax.named_scope("w2_fwd_wait"):
-        w2_fwd.wait_recv()
-
-    def partial_of(slot):
-        hidden = silu(INN[slot] * spread_two + offset_two).astype(BF16)
-        PT[slot] = jnp.dot(hidden, W2[...], preferred_element_type=F32)
+        spreads, offsets = [], []
+        for k in range(4):
+            piece = IST[0, :, k * HID : (k + 1) * HID]
+            for d in (1, 2, 3):
+                j = k ^ d
+                piece = piece + IST[d, :, j * HID : (j + 1) * HID]
+            one, two = affine(piece[0:1], piece[1:2], late_count, GI[k], SI[k])
+            spreads.append(one)
+            offsets.append(two)
+        spread_two = jnp.concatenate(spreads, axis=1)
+        offset_two = jnp.concatenate(offsets, axis=1)
+        for slot in range(NZ):
+            HB[slot] = silu(INN[slot] * spread_two + offset_two).astype(BF16)
+
+    def partial_of(slot, h):
+        at = half_cols[h]
+        PT[slot, :, at] = jnp.dot(HB[slot], W2[:, at], preferred_element_type=F32)
 
     sums_c, sums_a = {}, {}
 
-    def sum_hop(t, q):
+    ways = ((sums_c, SC, RC, 1), (sums_a, SA, RA, -1))
+
+    def sum_send(way, t, q, begin):
+        sums_d, S_, R_, step = way
         at = cols(q)
-        for slot, sums_d, S_, R_, step, half in (
-            (NZ - (H - t), sums_c, SC, RC, 1, q < Q // 2),
-            (H - t, sums_a, SA, RA, -1, q >= Q // 2),
-        ):
-            if t == 0 and not half:
-                continue
-            value = PT[slot, :, at]
-            if t > 1 or (t == 1 and half):
-                sums_d[t - 1, q].wait_recv()
-                value = value + R_[t - 1, :, at].astype(F32)
-            S_[t, :, at] = value.astype(BF16)
-            sums_d[t, q] = send(S_.at[t, :, at], R_.at[t, :, at], {"z": zat(step)})
+        value = PT[(step * (t - H)) % NZ, :, at]
+        if t > begin:
+            sums_d[t - 1, q].wait_recv()
+            value = value + R_[t - 1, :, at].astype(F32)
+        S_[t, :, at] = value.astype(BF16)
+        sums_d[t, q] = send(S_.at[t, :, at], R_.at[t, :, at], {"z": zat(step)})
+
+    def sum_begin(h):
+        late["fwd", h].wait_recv()
+        partial_of(H, h)
+        partial_of(H - 1 if h == 0 else H + 1, h)
+        for q in range(h * Q // 2, (h + 1) * Q // 2):
+            sum_send(ways[h], 0, q, 0)
+            sum_send(ways[1 - h], 1, q, 1)
+        for slot in range(NZ):
+            if slot not in (H, H - 1 if h == 0 else H + 1):
+                partial_of(slot, h)
+
+    def sum_hop(t, i):
+        begin = 0 if i >= Q // 2 else 1
+        sum_send(ways[0], t, (i + Q // 2) % Q, begin)
+        sum_send(ways[1], t, i, begin)
 
     def late_final(q):
         at = cols(q)
@@ -506,48 +551,24 @@
             value = value + RA[H - 1, :, at].astype(F32)
         LO[:, at] = (G[0, :, at].astype(F32) + value).astype(BF16)
 
-    def partials(t):
-        if t == 0:
-            partial_of(H)
-        elif t == H:
-            partial_of(0)
-        else:
-            partial_of(NZ - (H - t))
-            partial_of(H - t)
-
-    near_first = [d for d in order[::-1] if d]
-    side = [("early_two", functools.partial(early_two, p)) for p in range(EARLY_FIRST, PIECES)]
-    side += [("pair_send", functools.partial(pair_send, h, k)) for h in (0, 1) for k in (0, 1)]
-    side += [("x_send", functools.partial(x_send, k)) for k in (0, 1)]
-    side += [("z_send", functools.partial(z_send, k)) for k in (0, 1)]
-    side.append(("z_finish", z_finish))
-    side += [("z_forward", functools.partial(z_forward, d)) for d in near_first[:2]]
-    side.append(("across", functools.partial(back_across, 0)))
-    for at, d in enumerate(near_first[2:]):
-        side.append(("z_forward", functools.partial(z_forward, d)))
-        if at:
-            side.append(("across", functools.partial(back_across, -near_first[at - 1])))
-    main = [("partials", functools.partial(partials, 0))]
-    main += [("sum0", functools.partial(sum_hop, 0, q)) for q in range(Q)]
-    main += [("partials", functools.partial(partials, t)) for t in range(1, H + 1)]
-    main += [(f"sum{t}", functools.partial(sum_hop, t, q)) for t in range(1, H) for q in range(Q)]
-    main += [("late_final", functools.partial(late_final, q)) for q in range(Q)]
-    for step in PLAN:
-        which = main if step == "m" else side
-        if which:
-            name, go = which.pop(0)
-            with jax.named_scope(name):
-                go()
-    for name, go in main + side:
+    steps = {"I": second_norm, "ZF": z_finish, "A0": functools.partial(back_across, 0)}
+    for t in range(H + 1):
+        for i in range(Q):
+            steps[f"{t}{i}"] = functools.partial(sum_hop, t, i)
+            steps[f"{i}f"] = functools.partial(late_final, i)
+    for k in (0, 1):
+        steps[f"W{k}"] = functools.partial(second_weight, k)
+        steps[f"B{k}"] = functools.partial(sum_begin, k)
+        steps[f"Z{k}"] = functools.partial(z_send, k)
+    for t in range(1, H + 1):
+        steps[f"R{t}"] = functools.partial(z_forward, t)
+    for d in range(1, NZ):
+        steps[f"A{d}"] = functools.partial(back_across, d if d <= H else d - NZ)
+    for name in " ".join(PLAN).split():
         with jax.named_scope(name):
-            go()
-
-    with jax.named_scope("across"):
-        for d in near_first:
-            if -d not in c_back_two:
-                back_across(-d)
+            steps[name]()
     with jax.named_scope("c_back"):
-        for d in [0] + [-d for d in near_first]:
+        for d in c_back:
             c_back[d].wait_recv()
             c_back_two[d].wait_recv()
     with jax.named_scope("outputs"):
@@ -607,6 +628,7 @@
         VM((4, 1, HID), F32),
         VM((4, 2, 4 * HID), F32),
         VM((NZ, rows, 4 * HID), F32),
+        VM((NZ, rows, 4 * HID), BF16),
         VM((NZ, rows, CL), F32),
         VM((H, rows, CL), BF16),
         VM((H, rows, CL), BF16),

time: 86.4 us -> 81.4 us (0.942)
  Pallas kernels: 85.6 us -> 80.7 us
    pallas_call x1, Pallas kernels: 83.9 us -> 79 us  [shards(): pl.pallas_call(functools.partial(kernel, (NS, NZ)), out_shape=(VM((rows,...]
where the time goes in v3:
time: 81.4 us; the launch traced here: 81.3 us
  Pallas kernels  80.7 us (99%)
    pallas_call x1, Pallas kernels, shards(): pl.pallas_call(functools.partial(kernel, (NS, NZ)), out_shape=(VM((rows,...  79 us
    pallas_call x1, Pallas kernels, shards(): pl.pallas_call(place, out_shape=tuple((jax.ShapeDtypeStruct(x.shape, x.dt...  1.69 us

profile of v3, /device:TPU:1, one launch (start us, length us, event | category | flops | bytes accessed | tf_op | source)
XLA Modules:
  0.0 81.3 jit_solution(3145578769448818854)
XLA Ops:
  0.6 79.0 %relay_step.1 = (bf16[98,1024]{1,0:T(8,128)(2,1)S(1)}, bf16[1568,256]{1,0:T(8,128)(2,1)S(1)}, f32[256,1024]{1,0:T(8,128)S(1)}, f32[1024,256]{1,0:T(8,128)S(1)}) custom-call(bf16[98,1024]{1,0:T(8,128)(2,1)} %bitcast.17, bf16[98,1024]{1,0:T(8,128)(2,1)} %entry_ref.1, f32[1,1024]{1,0:T(1,128)} %gain_first_ref.1, f32[1,1024]{1,0:T(1,128)} %shift_first_ref.1, ...), custom_call_target="tpu_custom_call" | custom-call | tf_op jit(solution)/shard_map/relay_step/pallas_call | solution.py:656
  79.6 1.7 %place.1 = (bf16[98,1024]{1,0:T(8,128)(2,1)}, bf16[1568,256]{1,0:T(8,128)(2,1)}, f32[256,1024]{1,0:T(8,128)}, f32[1024,256]{1,0:T(8,128)}) custom-call(bf16[98,1024]{1,0:T(8,128)(2,1)S(1)} %get-tuple-element.12.refs_0_, bf16[1568,256]{1,0:T(8,128)(2,1)S(1)} %get-tuple-element.13.refs_1_, f32[256,1024]{1,0:T(8,128)S(1)} %get-tuple-element.14.refs_2_, ...), custom_call_target="tpu_custom_call" | custom-call | tf_op jit(solution)/shard_map/place/pallas_call | solution.py:692

commit v4 on v3

--- a/solution.py
+++ b/solution.py
@@ -21,13 +21,13 @@
 PLAN = (
     "Z0 Z1 I W0",
     "B0 ZF W1 B1",
-    "12 13 R1 A0",
-    "20 21 22 R2",
-    "A7 A1 23 30",
-    "31 R3 A6 A2",
-    "32 33 R4 A5",
-    "A3 0f 1f 2f",
-    "3f A4",
+    "12 13 R1 R2",
+    "A0 20 21 22",
+    "23 A7 A1 30",
+    "R3 R4 A6 A2",
+    "31 32 33 A5",
+    "A3 0f 1f A4",
+    "2f 3f",
 )
 FAR_FIRST = (4, 3, 5, 2, 6, 1, 7, 0)
 
@@ -100,6 +100,7 @@
 ):
     NS, NZ = sizes
     H = NZ // 2
+    assert H == 4
     rows, CL = S.shape
     CQ = CL // Q
     HID = expand_late_ref.shape[1]
@@ -357,7 +358,7 @@
         return pl.ds(pl.multiple_of(half * (CE // 2) + zat(d) * ZR, ZR), ZR)
 
     pair_sums, x_sums, z_sums, x_back, c_back, c_back_two = {}, {}, {}, {}, {}, {}
-    back_c, back_a = {}, {}
+    back = {}
     HALF = FE // 2
 
     def pair_send(h, k):
@@ -406,24 +407,28 @@
                 z_sums[d].wait_recv()
                 value = value + RZ[d].astype(F32)
         FIN[c, b, pl.ds(pl.multiple_of(z * ZR, ZR), ZR), :] = (value * factor).astype(BF16)
-        z_back(1)
+        for by in (1, -1, 2, -2):
+            z_back(by, 0, by)
         back_to_x_and_core(0)
 
-    def z_back(t):
-        for back, step in ((back_c, 1), (back_a, -1)):
-            piece = fin(c, b, -step * (t - 1))
-            if t == H:
-                piece = piece.at[:, 0:HALF] if step == 1 else piece.at[:, HALF:FE]
-            back[t] = send(piece, piece, {"z": zat(step)})
+    def z_back(key, d, by, at=slice(None)):
+        piece = fin(c, b, d).at[:, at]
+        back[key] = send(piece, piece, {"z": zat(by)})
 
     def z_forward(t):
-        back_c[t].wait_recv()
-        back_a[t].wait_recv()
         if t < H:
-            z_back(t + 1)
+            back[t].wait_recv()
+            back[-t].wait_recv()
+            if t == 2:
+                z_back(3, -2, 1)
+                z_back(-3, 2, -1)
+                z_back("c", -2, 2, slice(0, HALF))
+                z_back("a", 2, -2, slice(HALF, FE))
             back_to_x_and_core(-t)
             back_to_x_and_core(t)
         else:
+            back["c"].wait_recv()
+            back["a"].wait_recv()
             back_to_x_and_core(H)
 
     def both(*slots):

time: 81.4 us -> 80.7 us (level)
  no operation moved by 1% of the time
where the time goes in v4:
time: 80.7 us; the launch traced here: 80.6 us
  Pallas kernels  80 us (99%)
    pallas_call x1, Pallas kernels, shards(): pl.pallas_call(functools.partial(kernel, (NS, NZ)), out_shape=(VM((rows,...  78.3 us
    pallas_call x1, Pallas kernels, shards(): pl.pallas_call(place, out_shape=tuple((jax.ShapeDtypeStruct(x.shape, x.dt...  1.69 us

profile of v4, /device:TPU:1, one launch (start us, length us, event | category | flops | bytes accessed | tf_op | source)
XLA Modules:
  0.0 80.6 jit_solution(2122280267874870680)
XLA Ops:
  0.6 78.3 %relay_step.1 = (bf16[98,1024]{1,0:T(8,128)(2,1)S(1)}, bf16[1568,256]{1,0:T(8,128)(2,1)S(1)}, f32[256,1024]{1,0:T(8,128)S(1)}, f32[1024,256]{1,0:T(8,128)S(1)}) custom-call(bf16[98,1024]{1,0:T(8,128)(2,1)} %bitcast.17, bf16[98,1024]{1,0:T(8,128)(2,1)} %entry_ref.1, f32[1,1024]{1,0:T(1,128)} %gain_first_ref.1, f32[1,1024]{1,0:T(1,128)} %shift_first_ref.1, ...), custom_call_target="tpu_custom_call" | custom-call | tf_op jit(solution)/shard_map/relay_step/pallas_call | solution.py:661
  79.0 1.7 %place.1 = (bf16[98,1024]{1,0:T(8,128)(2,1)}, bf16[1568,256]{1,0:T(8,128)(2,1)}, f32[256,1024]{1,0:T(8,128)}, f32[1024,256]{1,0:T(8,128)}) custom-call(bf16[98,1024]{1,0:T(8,128)(2,1)S(1)} %get-tuple-element.12.refs_0_, bf16[1568,256]{1,0:T(8,128)(2,1)S(1)} %get-tuple-element.13.refs_1_, f32[256,1024]{1,0:T(8,128)S(1)} %get-tuple-element.14.refs_2_, ...), custom_call_target="tpu_custom_call" | custom-call | tf_op jit(solution)/shard_map/place/pallas_call | solution.py:697
